TPU v7x, 512 devices: a whole 4x4x16 slice. The times are simulated.
512 devices in a mesh: gx: 32 (over z, x_lo), gy: 16 (over y, x_hi, core).
Axes of the slice: x: 4 (x_hi: 2, x_lo: 2; x = x_hi * 2 + x_lo), y: 4, z: 16, core: 2. Of those that a mesh axis runs over, the one named last changes fastest.
Arguments:
- field: float32 [256, 128, 192], P('gx', 'gy'), may hold values from -6 to 6
- target: float32 [256, 128, 192], P('gx', 'gy'), may hold values from -6 to 6
- embed_weight: float32 [192, 256], replicated, may hold values from -0.4375 to 0.4375
- norm_gain: float32 [256], replicated, may hold values from 0.5 to 1.5
- attend_weight: float32 [256, 768], replicated, may hold values from -0.375 to 0.375
- output_weight: float32 [256, 256], replicated, may hold values from -0.375 to 0.375
- second_gain: float32 [256], replicated, may hold values from 0.5 to 1.5
- expand_weight: float32 [256, 512], replicated, may hold values from -0.375 to 0.375
- reduce_weight: float32 [512, 256], replicated, may hold values from -0.25 to 0.25
- decode_weight: float32 [256, 192], replicated, may hold values from -0.375 to 0.375
Outputs:
- loss: float32 [], replicated
- field_gradient: float32 [256, 128, 192], P('gx', 'gy')
- embed_gradient: float32 [192, 256], replicated
- norm_gradient: float32 [256], replicated
- attend_gradient: float32 [256, 768], replicated
- output_gradient: float32 [256, 256], replicated
- second_gradient: float32 [256], replicated
- expand_gradient: float32 [256, 512], replicated
- reduce_gradient: float32 [512, 256], replicated
- decode_gradient: float32 [256, 192], replicated
All inputs are finite; a program needn't handle non-finite values.
Results may differ from a plain program's by a relative error of at most 0.0001.
Values sent between devices are 32-bit elements; how exact they have to be, the bound alone decides.
No kernel may reach another device: no remote copies, remote signals or barrier semaphores. Data moves between devices by JAX's collectives and lax.ppermute only.
A program may use at most 128 MiB of HBM per device.

v0:
```python
import jax
import jax.numpy as jnp
from jax import lax
from jax.sharding import PartitionSpec as P

PATCH = 4
HEADS = 8
STEPS = 2


EXACT = lax.Precision.HIGHEST
EPSILON = 1e-06
TIME_STEP = 0.1
VISCOSITY = 0.5


def with_halo(x, sides, width):
    for axis, dim in sides:
        count, length = (lax.axis_size(axis), x.shape[dim])
        up = [(i, (i + 1) % count) for i in range(count)]
        down = [(j, i) for i, j in up]
        last = lax.slice_in_dim(x, length - width, length, axis=dim)
        leading = lax.slice_in_dim(x, 0, width, axis=dim)
        before = lax.ppermute(last, axis, up)
        after = lax.ppermute(leading, axis, down)
        x = jnp.concatenate([before, x, after], axis=dim)
    return x


def matmul(left, right):
    return jnp.dot(left, right, precision=EXACT)


def rms_scale(values, gain):
    power = jnp.mean(values * values, axis=-1, keepdims=True)
    return values * lax.rsqrt(power + EPSILON) * gain


def closure(ext, params):
    (
        embed_weight,
        norm_gain,
        attend_weight,
        output_weight,
        second_gain,
        expand_weight,
        reduce_weight,
        decode_weight,
    ) = params
    wide, tall, depth = ext.shape
    levels = depth // 3
    across, along, upward = (wide // PATCH, tall // PATCH, levels // PATCH)
    patches = ext.reshape(across, PATCH, along, PATCH, 3, upward, PATCH).transpose(
        0, 2, 5, 4, 1, 3, 6
    )
    patches = patches.reshape(across, along, upward, 3 * PATCH * PATCH * PATCH)
    tokens = matmul(patches, embed_weight)
    width = tokens.shape[-1]
    head_size = width // HEADS
    mixed = matmul(rms_scale(tokens, norm_gain), attend_weight)
    inner_x, inner_y = (across - 2, along - 2)
    queries = mixed[1:-1, 1:-1, :, :width].reshape(inner_x, inner_y, upward, HEADS, head_size)
    keyset = mixed[:, :, :, width : 2 * width]
    valset = mixed[:, :, :, 2 * width :]
    offsets = [(shift_x, shift_y) for shift_x in range(3) for shift_y in range(3)]
    keyblock = jnp.concatenate(
        [keyset[sx : sx + inner_x, sy : sy + inner_y] for sx, sy in offsets], axis=2
    )
    valblock = jnp.concatenate(
        [valset[sx : sx + inner_x, sy : sy + inner_y] for sx, sy in offsets], axis=2
    )
    keyblock = keyblock.reshape(inner_x, inner_y, 9 * upward, HEADS, head_size)
    valblock = valblock.reshape(inner_x, inner_y, 9 * upward, HEADS, head_size)
    factor = head_size ** (-0.5)
    scores = jnp.einsum("xyzhe,xywhe->xyhzw", queries, keyblock, precision=EXACT) * factor
    weights = jnp.exp(scores)
    weights = weights / jnp.sum(weights, axis=-1, keepdims=True)
    attended = jnp.einsum("xyhzw,xywhe->xyzhe", weights, valblock, precision=EXACT)
    attended = attended.reshape(inner_x, inner_y, upward, width)
    middle = tokens[1:-1, 1:-1] + matmul(attended, output_weight)
    hidden = jax.nn.silu(matmul(rms_scale(middle, second_gain), expand_weight))
    middle = middle + matmul(hidden, reduce_weight)
    result = matmul(middle, decode_weight).reshape(inner_x, inner_y, upward, 3, PATCH, PATCH, PATCH)
    return result.transpose(0, 4, 1, 5, 3, 2, 6).reshape(inner_x * PATCH, inner_y * PATCH, depth)


def advance(ext, params):
    wide, tall, depth = ext.shape
    levels = depth // 3
    inner = ext[PATCH : wide - PATCH, PATCH : tall - PATCH]
    east = ext[PATCH + 1 : wide - PATCH + 1, PATCH : tall - PATCH]
    west = ext[PATCH - 1 : wide - PATCH - 1, PATCH : tall - PATCH]
    north = ext[PATCH : wide - PATCH, PATCH + 1 : tall - PATCH + 1]
    south = ext[PATCH : wide - PATCH, PATCH - 1 : tall - PATCH - 1]
    level = jnp.arange(depth, dtype=jnp.int32) % levels
    blank = jnp.zeros(inner.shape[:2] + (1,), jnp.float32)
    upper = jnp.where(level == levels - 1, 0.0, jnp.concatenate([inner[:, :, 1:], blank], axis=2))
    lower = jnp.where(level == 0, 0.0, jnp.concatenate([blank, inner[:, :, :-1]], axis=2))
    laplace = east + west + north + south + upper + lower - 6.0 * inner
    speed_x = jnp.concatenate([inner[:, :, 0:levels]] * 3, axis=2)
    speed_y = jnp.concatenate([inner[:, :, levels : 2 * levels]] * 3, axis=2)
    speed_z = jnp.concatenate([inner[:, :, 2 * levels :]] * 3, axis=2)
    carried = 0.5 * (
        speed_x * (east - west) + speed_y * (north - south) + speed_z * (upper - lower)
    )
    return inner + TIME_STEP * (VISCOSITY * laplace - carried + closure(ext, params))


def fold(spread, margin):
    for axis_dim in (0, 1):
        length = spread.shape[axis_dim] - 4 * margin
        middle = lax.slice_in_dim(spread, 2 * margin, 2 * margin + length, axis=axis_dim)
        lowside = lax.slice_in_dim(spread, 0, margin, axis=axis_dim)
        highside = lax.slice_in_dim(spread, length + 3 * margin, length + 4 * margin, axis=axis_dim)
        pad_low = [(0, 0), (0, 0), (0, 0)]
        pad_high = [(0, 0), (0, 0), (0, 0)]
        pad_low[axis_dim] = (0, length - margin)
        pad_high[axis_dim] = (length - margin, 0)
        spread = middle + jnp.pad(lowside, pad_low) + jnp.pad(highside, pad_high)
    return spread


def shards(
    field,
    target,
    embed_weight,
    norm_gain,
    attend_weight,
    output_weight,
    second_gain,
    expand_weight,
    reduce_weight,
    decode_weight,
):
    params = (
        embed_weight,
        norm_gain,
        attend_weight,
        output_weight,
        second_gain,
        expand_weight,
        reduce_weight,
        decode_weight,
    )
    energy = lax.psum(jnp.sum(target * target), ("gx", "gy"))
    current = field
    pullbacks = []
    for step in range(STEPS):
        extended = with_halo(current, (("gx", 0), ("gy", 1)), PATCH)
        current, pullback = jax.vjp(advance, extended, params)
        pullbacks.append(pullback)
    residue = current - target
    cotangent = 2.0 * residue
    gradients = None
    for pullback in reversed(pullbacks):
        back_ext, back_params = pullback(cotangent)
        gradients = (
            back_params if gradients is None else jax.tree.map(jnp.add, gradients, back_params)
        )
        spread = with_halo(back_ext, (("gx", 0), ("gy", 1)), PATCH)
        cotangent = fold(spread, PATCH)
    local_misfit = jnp.sum(residue * residue)
    misfit = lax.psum(local_misfit, ("gx", "gy"))
    summed = lax.psum(tuple(gradients), ("gx", "gy"))
    entries = (
        field.shape[0] * lax.axis_size("gx") * field.shape[1] * lax.axis_size("gy") * field.shape[2]
    )
    scale = jnp.float32(entries) / energy
    loss = misfit / energy
    return (loss, scale * cotangent) + tuple((scale * piece for piece in summed))


def solution(mesh):
    in_specs = (P("gx", "gy", None), P("gx", "gy", None), P(), P(), P(), P(), P(), P(), P(), P())
    out_specs = (P(), P("gx", "gy", None), P(), P(), P(), P(), P(), P(), P(), P())
    return jax.shard_map(shards, mesh=mesh, in_specs=in_specs, out_specs=out_specs, check_vma=False)
```

profile of v0, /device:TPU:1, one launch (start us, length us, event | category | flops | bytes accessed | tf_op | source)
XLA Modules:
  0.0 810.8 jit_solution(4378260794345569212)
XLA Ops:
  8.1 12.9 %collective-permute-start = (f32[4,8,192]{2,1,0:T(8,128)S(1)}, f32[4,8,192]{2,1,0:T(8,128)S(1)}, u32[]{:S(2)}, u32[]{:S(2)}) collective-permute-start(f32[4,8,192]{2,1,0:T(8,128)S(1)} %get-tuple-element.154), channel_id=1, source_target_pairs={{16,0},{32,16},{48,32},{64,48},{80,64},{96,80},{112,96},{128,112},... | collective-permute-start | bytes 73736 | tf_op jit(solution)/shard_map/ppermute | solution.py:25
  20.9 1.9 collective-permute-start.1
  29.2 6.3 collective-permute-start.3
  35.5 1.9 collective-permute-start.2
  38.2 4.5 collective-permute-done.2
  43.3 5.0 reshape.216
  48.4 6.5 copy.78
  54.9 2.7 multiply_reduce_fusion.7
  67.5 2.2 copy.85
  72.3 1.9 collective-permute-start.5
  74.2 5.5 collective-permute-start.4
  80.7 3.0 collective-permute-start.7
  83.7 1.9 collective-permute-start.6
  86.4 4.5 collective-permute-done.6
  90.9 5.0 reshape.224
  96.0 7.0 copy.86
  103.0 3.9 multiply_reduce_fusion.6
  111.8 1.9 fusion.184
  115.0 2.4 copy.88
  117.4 2.3 convolution_bitcast_fusion.10
  124.0 2.2 copy.93
  127.4 1.9 negate_add_fusion.3
  129.3 2.4 negate_add_fusion.2
  133.4 1.9 copy.94
  135.3 1.9 fusion.73
  138.8 2.1 multiply_reduce_fusion.9
  141.7 2.1 multiply_reduce_fusion.1
  146.6 2.2 fusion.36
  154.1 3.2 fusion.169
  158.4 1.8 copy.185
  160.3 1.9 copy.184
  162.2 1.9 copy.183
  171.2 3.0 fusion.170
  176.0 1.9 copy.194
  177.9 1.9 copy.193
  179.8 1.8 copy.192
  181.7 1.9 copy.191
  191.8 6.1 copy.118
  198.1 5.1 reshape.239
  203.7 1.9 collective-permute-start.8
  205.6 5.6 collective-permute-start.9
  212.6 3.2 collective-permute-start.10
  215.8 4.0 collective-permute-start.11
  220.4 3.1 collective-permute-done.11
  229.3 2.2 convolution_bitcast_fusion.12
  246.0 3.0 fusion.167
  249.1 1.8 copy.196
  250.9 1.9 copy.203
  252.8 1.9 copy.202
  262.6 3.3 fusion.168
  265.8 1.9 copy.205
  267.7 1.9 copy.212
  269.6 1.8 copy.211
  273.3 1.9 copy.209
  289.5 2.2 fusion.6
  293.5 6.3 copy.143
  299.8 5.0 reshape.247
  306.0 1.9 collective-permute-start.12
  307.9 5.5 collective-permute-start.13
  313.4 107.6 %all-reduce.72 = (f32[]{:T(128)}, f32[]{:T(128)}, f32[256]{0:T(256)S(1)}, f32[256]{0:T(256)S(1)}) all-reduce(f32[]{:T(128)} %get-tuple-element.141, f32[]{:T(128)} %multiply_reduce_fusion.12, f32[256]{0:T(256)S(1)} %add.385, f32[256]{0:T(256)S(1)} %add.388), channel_id=1, replica_groups=mesh['gx'=32,'gy'=16] {'gx','gy'}, use_global_device_ids=true, to_apply=%region_7.8 | all-reduce | flops 514 | bytes 4112 | tf_op jit(solution)/shard_map/psum | solution.py:163
  422.3 3.5 collective-permute-start.14
  425.9 1.9 collective-permute-start.15
  429.7 3.6 collective-permute-done.15
  434.2 360.8 %all-reduce.76.cloned.1.call-done = (f32[192,256]{1,0:T(8,128)}, f32[256,768]{1,0:T(8,128)}, f32[256,256]{1,0:T(8,128)}, f32[256,512]{1,0:T(8,128)}, f32[512,256]{1,0:T(8,128)}, /*index=5*/f32[256,192]{0,1:T(8,128)}) async-done(((f32[192,256]{1,0:T(8,128)}, f32[256,768]{1,0:T(8,128)}, f32[256,256]{1,0:T(8,128)}, f32[256,512]{1,0:T(8,128)}, f32[512,256]{1,0:T(8,128)}, /*index=5*/f32[256,192]{0,1:T(8,128)}), ...) | async-done | bytes 2490384 | tf_op jit(solution)/shard_map/psum | solution.py:164
  (592 shorter events, 122.3 us)
Async XLA Ops:
  7.2 51.0 %copy-start = (f32[256,768]{1,0:T(8,128)S(1)}, f32[256,768]{1,0:T(8,128)}, u32[]{:S(2)}) copy-start(f32[256,768]{1,0:T(8,128)} %param.14) | copy-start | bytes 2359300
  7.2 787.8 %all-reduce.76.cloned.1.call-start = ((), (), s32[]{:S(2)}) async-start(), calls=%async_computation | async-start | bytes 4980736 | tf_op jit(solution)/shard_map/psum | solution.py:164
  8.1 20.5 %collective-permute-start = (f32[4,8,192]{2,1,0:T(8,128)S(1)}, f32[4,8,192]{2,1,0:T(8,128)S(1)}, u32[]{:S(2)}, u32[]{:S(2)}) collective-permute-start(f32[4,8,192]{2,1,0:T(8,128)S(1)} %get-tuple-element.154), channel_id=1, source_target_pairs={{16,0},{32,16},{48,32},{64,48},{80,64},{96,80},{112,96},{128,112},... | collective-permute-start | bytes 73736 | tf_op jit(solution)/shard_map/ppermute | solution.py:25
  20.9 6.8 collective-permute-start.1
  28.6 14.0 %copy-start.36 = (f32[16,8,192]{2,1,0:T(8,128)}, f32[16,8,192]{2,1,0:T(8,128)S(1)}, u32[]{:S(2)}) copy-start(f32[16,8,192]{2,1,0:T(8,128)S(1)} %constant_dynamic-update-slice_fusion) | copy-start | bytes 294916
  29.2 9.0 %collective-permute-start.3 = (f32[16,4,192]{2,1,0:T(4,128)S(1)}, f32[16,4,192]{2,1,0:T(4,128)S(1)}, u32[]{:S(2)}, u32[]{:S(2)}) collective-permute-start(f32[16,4,192]{2,1,0:T(4,128)S(1)} %get-tuple-element.122), channel_id=1, source_target_pairs={{0,1},{1,2},{2,3},{3,4},{4,5},{5,6},{6,7},{7,8},{8,9},{9,10},{10,1... | collective-permute-start | bytes 147464 | tf_op jit(solution)/shard_map/ppermute | solution.py:24
  35.5 7.1 collective-permute-start.2
  37.5 33.5 %copy-start.191 = (pred[192]{0:T(512)(128)(4,1)}, pred[192]{0:T(512)(128)(4,1)S(1)}, u32[]{:S(2)}) copy-start(pred[192]{0:T(512)(128)(4,1)S(1)} %get-tuple-element.177) | copy-start | bytes 580
  37.5 33.5 %copy-start.196 = (pred[192]{0:T(512)(128)(4,1)}, pred[192]{0:T(512)(128)(4,1)S(1)}, u32[]{:S(2)}) copy-start(pred[192]{0:T(512)(128)(4,1)S(1)} %get-tuple-element.176) | copy-start | bytes 580
  48.4 6.6 copy-start.33
  72.3 8.1 %collective-permute-start.5 = (f32[4,8,192]{2,1,0:T(8,128)S(1)}, f32[4,8,192]{2,1,0:T(8,128)S(1)}, u32[]{:S(2)}, u32[]{:S(2)}) collective-permute-start(f32[4,8,192]{2,1,0:T(8,128)S(1)} %get-tuple-element.147), channel_id=1, source_target_pairs={{0,16},{16,32},{32,48},{48,64},{64,80},{80,96},{96,112},{112,128},... | collective-permute-start | bytes 73736 | tf_op jit(solution)/shard_map/ppermute | solution.py:24
  74.2 6.5 collective-permute-start.4
  80.4 15.5 %copy-start.111 = (f32[4,8,192]{2,1,0:T(8,128)}, f32[4,8,192]{2,1,0:T(8,128)S(1)}, u32[]{:S(2)}) copy-start(f32[4,8,192]{2,1,0:T(8,128)S(1)} %collective-permute-done.5) | copy-start | bytes 73732
  80.7 15.3 %copy-start.113 = (f32[4,8,192]{2,1,0:T(8,128)}, f32[4,8,192]{2,1,0:T(8,128)S(1)}, u32[]{:S(2)}) copy-start(f32[4,8,192]{2,1,0:T(8,128)S(1)} %collective-permute-done.4) | copy-start | bytes 73732
  80.7 5.6 collective-permute-start.7
  83.7 7.1 collective-permute-start.6
  86.4 9.6 %copy-start.102 = (f32[16,4,192]{2,1,0:T(4,128)}, f32[16,4,192]{2,1,0:T(4,128)S(1)}, u32[]{:S(2)}) copy-start(f32[16,4,192]{2,1,0:T(4,128)S(1)} %collective-permute-done.7) | copy-start | bytes 147460
  113.8 6.0 copy-start.16
  135.3 5.6 copy-start.190
  135.3 5.7 copy-start.43
  135.3 5.7 copy-start.176
  135.3 5.7 copy-start.180
  135.3 5.8 copy-start.21
  135.3 6.3 copy-start.17
  160.3 9.3 %copy-start.46 = (f32[2,2,16,256]{2,3,1,0:T(8,128)S(1)}, f32[2,2,16,256]{2,3,1,0:T(8,128)}, u32[]{:S(2)}) copy-start(f32[2,2,16,256]{2,3,1,0:T(8,128)} %get-tuple-element.57) | copy-start | bytes 196612
  162.2 8.2 %copy-start.45 = (f32[2,2,16,256]{2,3,1,0:T(8,128)S(1)}, f32[2,2,16,256]{2,3,1,0:T(8,128)}, u32[]{:S(2)}) copy-start(f32[2,2,16,256]{2,3,1,0:T(8,128)} %get-tuple-element.58) | copy-start | bytes 196612
  176.0 9.4 %copy-start.49 = (f32[2,2,16,256]{2,3,1,0:T(8,128)S(1)}, f32[2,2,16,256]{2,3,1,0:T(8,128)}, u32[]{:S(2)}) copy-start(f32[2,2,16,256]{2,3,1,0:T(8,128)} %get-tuple-element.65) | copy-start | bytes 196612
  177.9 8.3 %copy-start.47 = (f32[2,2,16,256]{2,3,1,0:T(8,128)S(1)}, f32[2,2,16,256]{2,3,1,0:T(8,128)}, u32[]{:S(2)}) copy-start(f32[2,2,16,256]{2,3,1,0:T(8,128)} %get-tuple-element.66) | copy-start | bytes 196612
  190.3 7.7 copy-start.163
  198.1 5.5 copy-start.135
  203.2 8.1 copy-start.132
  203.2 16.6 %copy-start.155 = (f32[2,2,8,16]{3,2,1,0:T(8,128)S(1)}, f32[2,2,8,16]{3,2,1,0:T(8,128)}, u32[]{:S(2)}) copy-start(f32[2,2,8,16]{3,2,1,0:T(8,128)} %copy-done.154) | copy-start | bytes 6148
  203.5 20.1 %copy-start.194 = (pred[8]{0:T(512)(128)(4,1)S(1)}, pred[8]{0:T(512)(128)(4,1)}, u32[]{:S(2)}) copy-start(pred[8]{0:T(512)(128)(4,1)} %constant.73.clone.1) | copy-start | bytes 28
  203.7 20.0 %copy-start.108 = (f32[8,8,64]{2,1,0:T(8,128)S(1)}, f32[8,8,64]{2,1,0:T(8,128)}, u32[]{:S(2)}) copy-start(f32[8,8,64]{2,1,0:T(8,128)} %get-tuple-element.152) | copy-start | bytes 49156
  203.7 8.3 %collective-permute-start.8 = (f32[4,16,192]{2,1,0:T(8,128)S(1)}, f32[4,16,192]{2,1,0:T(8,128)S(1)}, u32[]{:S(2)}, u32[]{:S(2)}) collective-permute-start(f32[4,16,192]{2,1,0:T(8,128)S(1)} %get-tuple-element.112), channel_id=1, source_target_pairs={{0,16},{16,32},{32,48},{48,64},{64,80},{80,96},{96,112},{112,128},... | collective-permute-start | bytes 147464 | tf_op jit(solution)/shard_map/ppermute | solution.py:24
  205.6 6.9 collective-permute-start.9
  211.9 12.5 %copy-start.37 = (f32[16,8,192]{2,1,0:T(8,128)S(1)}, f32[16,8,192]{2,1,0:T(8,128)}, u32[]{:S(2)}) copy-start(f32[16,8,192]{2,1,0:T(8,128)} %copy-done.36) | copy-start | bytes 294916
  211.9 12.5 %copy-start.90 = (f32[8,8,191]{2,1,0:T(8,128)S(1)}, f32[8,8,191]{2,1,0:T(8,128)}, u32[]{:S(2)}) copy-start(f32[8,8,191]{2,1,0:T(8,128)} %get-tuple-element.149) | copy-start | bytes 146692
  211.9 12.5 %copy-start.91 = (f32[8,8,191]{2,1,0:T(8,128)S(1)}, f32[8,8,191]{2,1,0:T(8,128)}, u32[]{:S(2)}) copy-start(f32[8,8,191]{2,1,0:T(8,128)} %get-tuple-element.150) | copy-start | bytes 146692
  211.9 12.5 %copy-start.95 = (f32[16,4,192]{2,1,0:T(4,128)S(1)}, f32[16,4,192]{2,1,0:T(4,128)}, u32[]{:S(2)}) copy-start(f32[16,4,192]{2,1,0:T(4,128)} %copy-done.94) | copy-start | bytes 147460
  211.9 12.5 %copy-start.97 = (f32[16,4,192]{2,1,0:T(4,128)S(1)}, f32[16,4,192]{2,1,0:T(4,128)}, u32[]{:S(2)}) copy-start(f32[16,4,192]{2,1,0:T(4,128)} %copy-done.96) | copy-start | bytes 147460
  211.9 12.5 %copy-start.124 = (f32[4,8,192]{2,1,0:T(8,128)S(1)}, f32[4,8,192]{2,1,0:T(8,128)}, u32[]{:S(2)}) copy-start(f32[4,8,192]{2,1,0:T(8,128)} %copy-done.123) | copy-start | bytes 73732
  212.0 12.5 %copy-start.126 = (f32[4,8,192]{2,1,0:T(8,128)S(1)}, f32[4,8,192]{2,1,0:T(8,128)}, u32[]{:S(2)}) copy-start(f32[4,8,192]{2,1,0:T(8,128)} %copy-done.125) | copy-start | bytes 73732
  212.0 12.5 %copy-start.128 = (f32[8,8,64]{2,1,0:T(8,128)S(1)}, f32[8,8,64]{2,1,0:T(8,128)}, u32[]{:S(2)}) copy-start(f32[8,8,64]{2,1,0:T(8,128)} %get-tuple-element.153) | copy-start | bytes 49156
  212.0 12.5 %copy-start.197 = (pred[192]{0:T(512)(128)(4,1)S(1)}, pred[192]{0:T(512)(128)(4,1)}, u32[]{:S(2)}) copy-start(pred[192]{0:T(512)(128)(4,1)} %copy-done.196) | copy-start | bytes 580
  212.6 7.8 collective-permute-start.10
  215.8 7.7 collective-permute-start.11
  227.4 5.9 copy-start.188
  227.5 6.0 copy-start.22
  231.5 5.8 copy-start.14
  250.9 9.3 %copy-start.50 = (f32[2,2,16,256]{2,3,1,0:T(8,128)S(1)}, f32[2,2,16,256]{2,3,1,0:T(8,128)}, u32[]{:S(2)}) copy-start(f32[2,2,16,256]{2,3,1,0:T(8,128)} %get-tuple-element.38) | copy-start | bytes 196612
  252.8 8.2 %copy-start.48 = (f32[2,2,16,256]{2,3,1,0:T(8,128)S(1)}, f32[2,2,16,256]{2,3,1,0:T(8,128)}, u32[]{:S(2)}) copy-start(f32[2,2,16,256]{2,3,1,0:T(8,128)} %get-tuple-element.39) | copy-start | bytes 196612
  265.8 9.4 %copy-start.52 = (f32[2,2,16,256]{2,3,1,0:T(8,128)S(1)}, f32[2,2,16,256]{2,3,1,0:T(8,128)}, u32[]{:S(2)}) copy-start(f32[2,2,16,256]{2,3,1,0:T(8,128)} %get-tuple-element.46) | copy-start | bytes 196612
  267.7 8.3 %copy-start.51 = (f32[2,2,16,256]{2,3,1,0:T(8,128)S(1)}, f32[2,2,16,256]{2,3,1,0:T(8,128)}, u32[]{:S(2)}) copy-start(f32[2,2,16,256]{2,3,1,0:T(8,128)} %get-tuple-element.47) | copy-start | bytes 196612
  305.2 8.2 %copy-start.198 = (f32[256]{0:T(256)S(1)}, f32[256]{0:T(256)}, u32[]{:S(2)}) copy-start(f32[256]{0:T(256)} %get-tuple-element.16) | copy-start | bytes 3076
  305.2 8.2 %copy-start.200 = (f32[256]{0:T(256)S(1)}, f32[256]{0:T(256)}, u32[]{:S(2)}) copy-start(f32[256]{0:T(256)} %get-tuple-element.14) | copy-start | bytes 3076
  305.2 8.2 %copy-start.199 = (f32[256]{0:T(256)S(1)}, f32[256]{0:T(256)}, u32[]{:S(2)}) copy-start(f32[256]{0:T(256)} %get-tuple-element.12) | copy-start | bytes 3076
  305.2 8.2 %copy-start.201 = (f32[256]{0:T(256)S(1)}, f32[256]{0:T(256)}, u32[]{:S(2)}) copy-start(f32[256]{0:T(256)} %get-tuple-element.10) | copy-start | bytes 3076
  305.2 128.2 %copy-start.195 = (pred[8]{0:T(512)(128)(4,1)S(1)}, pred[8]{0:T(512)(128)(4,1)}, u32[]{:S(2)}) copy-start(pred[8]{0:T(512)(128)(4,1)} %constant.73.clone.1) | copy-start | bytes 28
  306.0 116.3 %collective-permute-start.12 = (f32[4,16,192]{2,1,0:T(8,128)S(1)}, f32[4,16,192]{2,1,0:T(8,128)S(1)}, u32[]{:S(2)}, u32[]{:S(2)}) collective-permute-start(f32[4,16,192]{2,1,0:T(8,128)S(1)} %get-tuple-element.110), channel_id=1, source_target_pairs={{0,16},{16,32},{32,48},{48,64},{64,80},{80,96},{96,112},{112,128},... | collective-permute-start | bytes 147464 | tf_op jit(solution)/shard_map/ppermute | solution.py:24
  307.9 114.4 %collective-permute-start.13 = (f32[4,16,192]{2,1,0:T(8,128)S(1)}, f32[4,16,192]{2,1,0:T(8,128)S(1)}, u32[]{:S(2)}, u32[]{:S(2)}) collective-permute-start(f32[4,16,192]{2,1,0:T(8,128)S(1)} %get-tuple-element.111), channel_id=1, source_target_pairs={{16,0},{32,16},{48,32},{64,48},{80,64},{96,80},{112,96},{128,112},... | collective-permute-start | bytes 147464 | tf_op jit(solution)/shard_map/ppermute | solution.py:25
  422.3 7.4 collective-permute-start.14
  425.9 7.4 collective-permute-start.15
  795.0 5.9 copy-start.115
  (157 other events, 467.8 us)
Sparse Core Ops, SparseCore 0:
  305.3 489.6 all-reduce.75
where the time goes:
time: 823 us; the launch traced here: 811 us
  waiting for transfers between devices  379 us (46%)
  local copies, waits for them, and re-layouts  147 us (18%)
  blocking collectives  108 us (13%)
  matrix products  67.6 us (8%)
  starting transfers between devices  63 us (8%)
  other arithmetic  26.2 us (3%)
  between operations  20.3 us (2%)
    psum x1, waiting for transfers between devices, shards(): summed = lax.psum(tuple(gradients), ('gx', 'gy'))  361 us
    psum x1, blocking collectives, shards(): misfit = lax.psum(local_misfit, ('gx', 'gy'))  108 us
    unnamed x462, local copies, waits for them, and re-layouts  58.7 us
    dot_general x36, matrix products, matmul(): return jnp.dot(left, right, precision=EXACT)  49.2 us
    ppermute x8, starting transfers between devices, with_halo(): after = lax.ppermute(leading, axis, down)  39.2 us
    transpose x4, local copies, waits for them, and re-layouts, closure(): ext.reshape(across, PATCH, along, PATCH, 3, upward, PATCH)  25.9 us
    ppermute x8, starting transfers between devices, with_halo(): before = lax.ppermute(last, axis, up)  23.7 us
    reshape x4, local copies, waits for them, and re-layouts, closure(): ext.reshape(across, PATCH, along, PATCH, 3, upward, PATCH)  20.2 us
  transfers between devices with their start and end apart: 17, of which 8 were waited for; matrix products, arithmetic and copies ran while one was open for 1% of the time, Pallas kernels for 0%

commit v1 on v0

v1 whole, which is shorter than its diff:
```python
import jax
import jax.numpy as jnp
from jax import lax
from jax.experimental import pallas as pl
from jax.experimental.pallas import tpu as pltpu
from jax.sharding import Mesh, PartitionSpec as P

F32 = jnp.float32
BF16 = jnp.bfloat16
EPSILON = 1e-06
FACTOR = 32 ** (-0.5)
INTERPRET = False

EMBED, ATTEND, OUTPUT, EXPAND, REDUCE, DECODE, SMALL, ROWS = 0, 192, 960, 1216, 1728, 2240, 2432, 2560
VMEM_LIMIT = 60 * 1024 * 1024


def split(x):
    high = x.astype(BF16)
    return high, (x - high.astype(F32)).astype(BF16)


def dot(a, b, ca=1, cb=0):
    dims = (((ca,), (cb,)), ((), ()))

    def one(left, right):
        return lax.dot_general(left, right, dims, preferred_element_type=F32)

    return one(a[0], b[0]) + (one(a[0], b[1]) + one(a[1], b[0]))


def lanes(shape):
    return lax.broadcasted_iota(jnp.int32, shape, 1)


def over_components(x):
    x = x + pltpu.roll(x, 128, 1)
    return x + pltpu.roll(x, 64, 1)


def to_tokens(block_ref, rows_ref, turned_ref, out_ref):
    for px in range(2):
        for py in range(2):
            for dx in range(4):
                row = (px * 2 + py) * 16 + dx * 4
                rows_ref[row : row + 4, :] = block_ref[px * 4 + dx, py * 4 : py * 4 + 4, :]
    turned_ref[:, 0:64] = rows_ref[...].T
    turned_ref[:, 64:128] = jnp.zeros((192, 64), F32)
    lane = lanes((16, 128))
    halves = [[jnp.zeros((16, 128), F32) for _ in range(2)] for _ in range(4)]
    for c in range(3):
        for dz in range(4):
            piece = turned_ref[pl.ds(c * 64 + dz, 16, stride=4), :]
            place = c * 64 + dz * 16
            half, low = place // 128, place % 128
            chosen = (lane >= low) & (lane < low + 16)
            for column in range(4):
                shift = (low - column * 16) % 128
                moved = pltpu.roll(piece, shift, 1) if shift else piece
                halves[column][half] = jnp.where(chosen, moved, halves[column][half])
    for column in range(4):
        for half in range(2):
            out_ref[column * 16 : column * 16 + 16, half * 128 : half * 128 + 128] = halves[column][half]


def prepare_kernel(field_ref, target_ref, tokens_ref, goal_ref, rows_ref, turned_ref):
    to_tokens(field_ref, rows_ref, turned_ref, tokens_ref)
    to_tokens(target_ref, rows_ref, turned_ref, goal_ref)


def restore_kernel(a_ref, b_ref, c_ref, out_ref, turned_ref, rows_ref):
    total = a_ref[...] + (b_ref[...] + c_ref[...])
    lane = lanes((16, 128))
    for c in range(3):
        for dz in range(4):
            place = c * 64 + dz * 16
            half, low = place // 128, place % 128
            piece = jnp.zeros((16, 128), F32)
            for column in range(4):
                source = total[column * 16 : column * 16 + 16, half * 128 : half * 128 + 128]
                shift = (column * 16 - low) % 128
                moved = pltpu.roll(source, shift, 1) if shift else source
                chosen = (lane >= column * 16) & (lane < column * 16 + 16)
                piece = jnp.where(chosen, moved, piece)
            turned_ref[pl.ds(c * 64 + dz, 16, stride=4), :] = piece
    rows_ref[...] = turned_ref[...].T
    for px in range(2):
        for py in range(2):
            for dx in range(4):
                row = (px * 2 + py) * 16 + dx * 4
                out_ref[px * 4 + dx, py * 4 : py * 4 + 4, :] = rows_ref[row : row + 4, :]


def inner_rows(ref, m, n, dx=0, dy=0):
    width = ref.shape[1]
    parts = [ref[((X + 1 + dx) * m + 1 + dy) * 16 : ((X + 1 + dx) * m + 1 + dy + n) * 16, :] for X in range(n)]
    return jnp.concatenate(parts, axis=0)


def add_inner(ref, m, n, value, dx=0, dy=0):
    for X in range(n):
        start = ((X + 1 + dx) * m + 1 + dy) * 16
        ref[start : start + n * 16, :] += value[X * n * 16 : (X + 1) * n * 16]


def neighbours(ext_ref, m, n):
    count = n * n * 16
    lane = lanes((count, 256))
    row = lax.broadcasted_iota(jnp.int32, (count, 256), 0)
    dx, dy, dz, pz = (lane // 4) % 4, lane % 4, (lane // 16) % 4, row % 16
    here = inner_rows(ext_ref, m, n)
    roll = pltpu.roll
    east = jnp.where(dx < 3, roll(here, 252, 1), roll(inner_rows(ext_ref, m, n, 1, 0), 12, 1))
    west = jnp.where(dx > 0, roll(here, 4, 1), roll(inner_rows(ext_ref, m, n, -1, 0), 244, 1))
    north = jnp.where(dy < 3, roll(here, 255, 1), roll(inner_rows(ext_ref, m, n, 0, 1), 3, 1))
    south = jnp.where(dy > 0, roll(here, 1, 1), roll(inner_rows(ext_ref, m, n, 0, -1), 253, 1))
    above = jnp.where(pz == 15, 0.0, roll(here, count - 1, 0))
    below = jnp.where(pz == 0, 0.0, roll(here, 1, 0))
    upper = jnp.where(dz < 3, roll(here, 240, 1), roll(above, 48, 1))
    lower = jnp.where(dz > 0, roll(here, 16, 1), roll(below, 208, 1))
    speeds = [over_components(jnp.where(lane // 64 == k, here, 0.0)) for k in range(3)]
    return here, (east, west, north, south, upper, lower), speeds


def stencil(ext_ref, m, n):
    here, (east, west, north, south, upper, lower), speeds = neighbours(ext_ref, m, n)
    laplace = (east + west) + (north + south) + (upper + lower) - 6.0 * here
    carried = speeds[0] * (east - west) + speeds[1] * (north - south) + speeds[2] * (upper - lower)
    return here + 0.05 * (laplace - carried)


def stencil_back(ext_ref, back_ref, g, m, n):
    count = n * n * 16
    lane = lanes((count, 256))
    row = lax.broadcasted_iota(jnp.int32, (count, 256), 0)
    dx, dy, dz, pz = (lane // 4) % 4, lane % 4, (lane // 16) % 4, row % 16
    comp = lane // 64
    roll = pltpu.roll
    here, (east, west, north, south, upper, lower), speeds = neighbours(ext_ref, m, n)
    scaled = 0.05 * g
    own = 0.7 * g
    for k, (ahead, behind) in enumerate(((east, west), (north, south), (upper, lower))):
        own = own - jnp.where(comp == k, over_components(scaled * (ahead - behind)), 0.0)
    plus, minus = scaled * (1.0 - speeds[0]), scaled * (1.0 + speeds[0])
    own = own + jnp.where(dx > 0, roll(plus, 4, 1), 0.0) + jnp.where(dx < 3, roll(minus, 252, 1), 0.0)
    add_inner(back_ref, m, n, jnp.where(dx == 0, roll(plus, 244, 1), 0.0), 1, 0)
    add_inner(back_ref, m, n, jnp.where(dx == 3, roll(minus, 12, 1), 0.0), -1, 0)
    plus, minus = scaled * (1.0 - speeds[1]), scaled * (1.0 + speeds[1])
    own = own + jnp.where(dy > 0, roll(plus, 1, 1), 0.0) + jnp.where(dy < 3, roll(minus, 255, 1), 0.0)
    add_inner(back_ref, m, n, jnp.where(dy == 0, roll(plus, 253, 1), 0.0), 0, 1)
    add_inner(back_ref, m, n, jnp.where(dy == 3, roll(minus, 3, 1), 0.0), 0, -1)
    plus, minus = scaled * (1.0 - speeds[2]), scaled * (1.0 + speeds[2])
    own = own + jnp.where(dz > 0, roll(plus, 16, 1), 0.0) + jnp.where(dz < 3, roll(minus, 240, 1), 0.0)
    across = jnp.where(dz == 0, roll(plus, 208, 1), 0.0)
    own = own + jnp.where(pz == 0, 0.0, roll(across, 1, 0))
    across = jnp.where(dz == 3, roll(minus, 48, 1), 0.0)
    own = own + jnp.where(pz == 15, 0.0, roll(across, count - 1, 0))
    add_inner(back_ref, m, n, own)


def rms(x):
    return lax.rsqrt(jnp.mean(x * x, axis=1, keepdims=True) + EPSILON)


def rms_back(values, scale, gain, cotangent):
    weighted = cotangent * gain
    shared = jnp.mean(weighted * values, axis=1, keepdims=True)
    return scale * (weighted - values * (scale * scale * shared))


def pair(ref, start, size):
    return ref[0, pl.ds(start, size), :], ref[1, pl.ds(start, size), :]


def put(ref, start, value):
    high, low = split(value)
    ref[0, pl.ds(start, value.shape[0]), :] = high
    ref[1, pl.ds(start, value.shape[0]), :] = low


def both(ref):
    return ref[0], ref[1]


def head_mask():
    row = lax.broadcasted_iota(jnp.int32, (128, 256), 0)
    return row // 16 == lanes((128, 256)) // 32


def by_head(x, mask):
    wide = jnp.where(mask, jnp.concatenate([x] * 8, axis=0), 0.0)
    return split(wide)


def from_heads(x, mask):
    kept = jnp.where(mask, x, 0.0)
    total = kept[0:16]
    for head in range(1, 8):
        total = total + kept[head * 16 : head * 16 + 16]
    return total


def key_rows(X, Y, m):
    return [pl.multiple_of(((X + dx) * m + Y) * 16, 16) for dx in range(3)]


def gather(ref, starts, low, high):
    def one(which):
        return jnp.concatenate([ref[which, pl.ds(s, 48), low:high] for s in starts], axis=0)

    return one(0), one(1)


def forward(w, g1, g2, ext_ref, r, m, n, chunk):
    (tok, nrm, kv, q, wts, att, mid, h, late) = r

    def embed(i, _):
        start = pl.multiple_of(i * chunk, chunk)
        tokens = dot(split(ext_ref[pl.ds(start, chunk), :]), both(w["embed"]))
        tok[pl.ds(start, chunk), :] = tokens
        normed = tokens * rms(tokens) * g1
        put(nrm, start, normed)
        put(kv, start, dot(pair(nrm, start, chunk), (w["attend"][0, :, 256:], w["attend"][1, :, 256:])))
        return 0

    lax.fori_loop(0, m * m * 16 // chunk, embed, 0)
    normed_in = inner_rows(nrm.at[0], m, n), inner_rows(nrm.at[1], m, n)
    q[...] = dot(normed_in, (w["attend"][0, :, :256], w["attend"][1, :, :256]))
    mask = head_mask()

    def attend(i, _):
        X, Y = i // n, i % n
        starts = key_rows(X, Y, m)
        here = pl.multiple_of(i * 16, 16)
        wide = by_head(q[pl.ds(here, 16), :], mask)
        scores = dot(gather(kv, starts, 0, 256), wide, 1, 1)
        weights = jnp.exp(scores * FACTOR)
        weights = weights / jnp.sum(weights, axis=0, keepdims=True)
        wts[i] = weights
        att[pl.ds(here, 16), :] = from_heads(dot(split(weights), gather(kv, starts, 256, 512), 0, 0), mask)
        return 0

    lax.fori_loop(0, n * n, attend, 0)
    middle = inner_rows(tok, m, n) + dot(split(att[...]), both(w["output"]))
    mid[...] = middle
    hidden = dot(split(middle * rms(middle) * g2), both(w["expand"]))
    h[...] = hidden
    active = hidden / (1.0 + jnp.exp(-hidden))
    final = middle + dot(split(active), both(w["reduce"]))
    late[...] = final
    return dot(split(final), both(w["decode"]), 1, 1)


def add_rows(ref, start, value, first):
    size = value.shape[0]
    if first:
        ref[start : start + size, :] = value
    else:
        ref[start : start + size, :] += value


def reorder(strip, source, inverse=False):
    places = [(c * 64 + dz * 16, c * 64 + dz) for c in range(3) for dz in range(4)]
    halves = []
    for k in range(2):
        part = source[:, 128 * k : 128 * k + 128]
        if inverse:
            for place, row in places:
                strip[k, pl.ds(row, 16, stride=4), :] = part[place : place + 16]
            halves.append(strip[k])
        else:
            strip[k] = part
            halves.append(jnp.concatenate([strip[k, pl.ds(row, 16, stride=4), :] for _, row in places], axis=0))
    return jnp.concatenate(halves, axis=1)


def backward(w, g1, g2, ext_ref, back_ref, grads, r, dkv, dq, g, m, n, chunk, first):
    (tok, nrm, kv, q, wts, att, mid, h, late) = r
    dclosure = split(0.1 * g)
    add_rows(grads, DECODE, dot(dclosure, split(late[...]), 0, 0)[:192], first)
    dmid = dot(dclosure, both(w["decode"]))
    back = split(dmid)
    hidden = h[...]
    gate = 1.0 / (1.0 + jnp.exp(-hidden))
    add_rows(grads, REDUCE, dot(split(hidden * gate), back, 0, 0), first)
    dhidden = split(dot(back, both(w["reduce"]), 1, 1) * (gate * (1.0 + hidden * (1.0 - gate))))
    middle = mid[...]
    scale = rms(middle)
    second = split(middle * scale * g2)
    add_rows(grads, EXPAND, dot(second, (dhidden[0][:, :256], dhidden[1][:, :256]), 0, 0), first)
    add_rows(grads, EXPAND + 256, dot(second, (dhidden[0][:, 256:], dhidden[1][:, 256:]), 0, 0), first)
    dsecond = dot(dhidden, both(w["expand"]), 1, 1)
    add_rows(grads, SMALL + 1, jnp.sum(dsecond * middle * scale, axis=0, keepdims=True), first)
    dmid = dmid + rms_back(middle, scale, g2, dsecond)
    back = split(dmid)
    add_rows(grads, OUTPUT, dot(split(att[...]), back, 0, 0), first)
    att[...] = dot(back, both(w["output"]), 1, 1)
    dkv[...] = jnp.zeros(dkv.shape, F32)
    mask = head_mask()

    def attend(i, _):
        X, Y = i // n, i % n
        starts = key_rows(X, Y, m)
        here = pl.multiple_of(i * 16, 16)
        wide = by_head(q[pl.ds(here, 16), :], mask)
        dwide = by_head(att[pl.ds(here, 16), :], mask)
        weights = wts[i]
        dweights = dot(gather(kv, starts, 256, 512), dwide, 1, 1)
        common = jnp.sum(weights * dweights, axis=0, keepdims=True)
        dscores = split(weights * (dweights - common) * FACTOR)
        dq[pl.ds(here, 16), :] = from_heads(dot(dscores, gather(kv, starts, 0, 256), 0, 0), mask)
        dkeys = dot(dscores, wide)
        dvals = dot(split(weights), dwide)
        for k, s in enumerate(starts):
            dkv[pl.ds(s, 48), 0:256] += dkeys[k * 48 : k * 48 + 48]
            dkv[pl.ds(s, 48), 256:512] += dvals[k * 48 : k * 48 + 48]
        return 0

    lax.fori_loop(0, n * n, attend, 0)
    normed_in = inner_rows(nrm.at[0], m, n), inner_rows(nrm.at[1], m, n)
    dquery = split(dq[...])
    add_rows(grads, ATTEND, dot(normed_in, dquery, 0, 0), first)
    back_ref[...] = jnp.zeros(back_ref.shape, F32)
    add_inner(back_ref, m, n, dot(dquery, (w["attend"][0, :, :256], w["attend"][1, :, :256]), 1, 1))
    total = dkv[...]
    halves = [split(total[:, 0:256]), split(total[:, 256:512])]
    normed = both(nrm)
    for k in range(2):
        add_rows(grads, ATTEND + 256 + 256 * k, dot(normed, halves[k], 0, 0), first)
    dnormed = back_ref[...]
    for k in range(2):
        low, high = 256 + 256 * k, 512 + 256 * k
        dnormed = dnormed + dot(halves[k], (w["attend"][0, :, low:high], w["attend"][1, :, low:high]), 1, 1)
    tokens = tok[...]
    scale = rms(tokens)
    add_rows(grads, SMALL, jnp.sum(dnormed * tokens * scale, axis=0, keepdims=True), first)
    back_ref[...] = rms_back(tokens, scale, g1, dnormed)
    add_inner(back_ref, m, n, dmid)
    dtokens = split(back_ref[...])
    add_rows(grads, EMBED, dot(split(ext_ref[...]), dtokens, 0, 0)[:192], first)
    back_ref[...] = dot(dtokens, both(w["embed"]), 1, 1)
    stencil_back(ext_ref, back_ref, g, m, n)


def main_kernel(*refs):
    (low, own, high, goal, embed, gain1, attend, output, gain2, expand, reduce, decode) = refs[:12]
    (grads, out_low, out_own, out_high) = refs[12:16]
    scratch = list(refs[16:])
    w = {}
    for name in ("embed", "attend", "output", "expand", "reduce", "decode"):
        w[name] = scratch.pop(0)
    strip = scratch.pop(0)
    ext0, back0, ext1, back1, dkv0, dkv1, dq0, dq1 = scratch[:8]
    r0, r1 = scratch[8:17], scratch[17:26]
    put(w["embed"], 0, reorder(strip, embed[...]))
    put(w["decode"], 0, reorder(strip, decode[...].T))
    put(w["embed"], 192, jnp.zeros((64, 256), F32))
    put(w["decode"], 192, jnp.zeros((64, 256), F32))
    put(w["attend"], 0, attend[...])
    put(w["output"], 0, output[...])
    put(w["expand"], 0, expand[...])
    put(w["reduce"], 0, reduce[...])
    g1, g2 = gain1[...], gain2[...]
    places = [
        (by, bx, (px * 2 + py) * 16, ((2 * bx + px) * 6 + 2 * by + py) * 16)
        for by in range(3) for bx in range(3) for px in range(2) for py in range(2)
    ]
    for by, bx, source, place in places:
        ext0[place : place + 16, :] = (low, own, high)[by][bx, source : source + 16, :]
    ext1[...] = stencil(ext0, 6, 4) + 0.1 * forward(w, g1, g2, ext0, r0, 6, 4, 192)
    final = stencil(ext1, 4, 2) + 0.1 * forward(w, g1, g2, ext1, r1, 4, 2, 128)
    residue = final - goal[...]
    grads[SMALL:ROWS, :] = jnp.zeros((ROWS - SMALL, 256), F32)
    sums = [jnp.sum(jnp.sum(v * v, axis=0, keepdims=True), axis=1, keepdims=True) for v in (residue, goal[...])]
    lane = lanes((1, 256))
    grads[SMALL + 2 : SMALL + 3, :] = jnp.where(lane == 0, sums[0], jnp.where(lane == 1, sums[1], 0.0))
    backward(w, g1, g2, ext1, back1, grads, r1, dkv1, dq1, 2.0 * residue, 4, 2, 128, True)
    backward(w, g1, g2, ext0, back0, grads, r0, dkv0, dq0, back1[...], 6, 4, 192, False)
    for by, bx, source, place in places:
        (out_low, out_own, out_high)[by][bx, source : source + 16, :] = back0[place : place + 16, :]


def finish_kernel(core, mine, other, loss, embed, norm, attend, output, second, expand, reduce, decode, strip, red):
    first = core[0] == 0
    red[0 : ROWS // 2, :] = jnp.where(first, mine[...], other[...])
    red[ROWS // 2 :, :] = jnp.where(first, other[...], mine[...])
    misfit = red[SMALL + 2 : SMALL + 3, 0:1]
    energy = red[SMALL + 2 : SMALL + 3, 1:2]
    scale = 6291456.0 / energy
    loss[...] = jnp.where(lanes((1, 128)) == 0, misfit / energy, scale)
    embed[...] = scale * reorder(strip, red[EMBED:ATTEND, :], True)
    for k in range(3):
        attend[:, 256 * k : 256 * k + 256] = scale * red[ATTEND + 256 * k : ATTEND + 256 * k + 256, :]
    output[...] = scale * red[OUTPUT:EXPAND, :]
    for k in range(2):
        expand[:, 256 * k : 256 * k + 256] = scale * red[EXPAND + 256 * k : EXPAND + 256 * k + 256, :]
    reduce[...] = scale * red[REDUCE:DECODE, :]
    decode[...] = (scale * reorder(strip, red[DECODE:SMALL, :], True)).T
    norm[...] = scale * red[SMALL : SMALL + 1, :]
    second[...] = scale * red[SMALL + 1 : SMALL + 2, :]


def arr(*shape, dtype=F32):
    return jax.ShapeDtypeStruct(shape, dtype)


def call(kernel, outs, scratch, name, **more):
    return pl.pallas_call(
        kernel,
        out_shape=outs,
        scratch_shapes=scratch,
        compiler_params=pltpu.CompilerParams(vmem_limit_bytes=VMEM_LIMIT),
        name=name,
        interpret=INTERPRET,
        **more,
    )


def prepare(field, target):
    scratch = [pltpu.VMEM((64, 192), F32), pltpu.VMEM((192, 128), F32)]
    return call(prepare_kernel, (arr(64, 256), arr(64, 256)), scratch, "prepare")(field, target)


def work(low, own, high, goal, weights):
    def V(*shape, dtype=F32):
        return pltpu.VMEM(shape, dtype)

    def kept(te, ti, n):
        return [
            V(te, 256), V(2, te, 256, dtype=BF16), V(2, te, 512, dtype=BF16), V(ti, 256), V(n * n, 144, 128),
            V(ti, 256), V(ti, 256), V(ti, 512), V(ti, 256),
        ]

    scratch = [
        V(2, 256, 256, dtype=BF16), V(2, 256, 768, dtype=BF16), V(2, 256, 256, dtype=BF16),
        V(2, 256, 512, dtype=BF16), V(2, 512, 256, dtype=BF16), V(2, 256, 256, dtype=BF16),
        V(2, 192, 128),
        V(576, 256), V(576, 256), V(256, 256), V(256, 256), V(576, 512), V(256, 512), V(256, 256), V(64, 256),
        *kept(576, 256, 4), *kept(256, 64, 2),
    ]
    outs = (arr(ROWS, 256), arr(3, 64, 256), arr(3, 64, 256), arr(3, 64, 256))
    embed, gain1, attend, output, gain2, expand, reduce, decode = weights
    args = (embed, gain1.reshape(1, 256), attend, output, gain2.reshape(1, 256), expand, reduce, decode)
    return call(main_kernel, outs, scratch, "work")(low, own, high, goal, *args)


def restore(a, b, c):
    scratch = [pltpu.VMEM((192, 128), F32), pltpu.VMEM((128, 192), F32)]
    return call(restore_kernel, arr(8, 8, 192), scratch, "restore")(a, b, c)


def finish(mine, other, core):
    outs = (
        arr(1, 128), arr(192, 256), arr(1, 256), arr(256, 768), arr(256, 256), arr(1, 256), arr(256, 512),
        arr(512, 256), arr(256, 192),
    )
    scratch = [pltpu.VMEM((2, 192, 128), F32), pltpu.VMEM((ROWS, 256), F32)]
    specs = [pl.BlockSpec(memory_space=pltpu.SMEM)] + [pl.BlockSpec(memory_space=pltpu.VMEM)] * 2
    return call(finish_kernel, outs, scratch, "finish", in_specs=specs)(core, mine, other)


AXES = ("z", "xl", "y", "xh", "co")
GX, GY = ("z", "xl"), ("y", "xh", "co")


def shift(x, axes, step):
    count = lax.axis_size(axes)
    return lax.ppermute(x, axes, [(i, (i + step) % count) for i in range(count)])


PLANE = ("xl", "y", "xh")


def swap(x, axes):
    return lax.all_to_all(x, axes, 0, 0, tiled=True)


def reduce_all(grads):
    core = lax.axis_index("co")
    halves = grads.reshape(2, ROWS // 2, 256)
    kept = lax.dynamic_index_in_dim(halves, core, 0, keepdims=False)
    sent = lax.dynamic_index_in_dim(halves, 1 - core, 0, keepdims=False)
    total = kept + lax.ppermute(sent, "co", [(0, 1), (1, 0)])
    total = jnp.sum(swap(total.reshape(16, ROWS // 32, 256), PLANE), axis=0)
    total = jnp.sum(swap(total.reshape(16, ROWS // 512, 256), "z"), axis=0)
    total = swap(jnp.broadcast_to(total, (16,) + total.shape), "z").reshape(ROWS // 32, 256)
    total = swap(jnp.broadcast_to(total, (16,) + total.shape), PLANE).reshape(ROWS // 2, 256)
    return total, lax.ppermute(total, "co", [(0, 1), (1, 0)])


def shards(field, target, *weights):
    tokens, goal = prepare(field, target)
    own = jnp.stack([shift(tokens, GX, 1), tokens, shift(tokens, GX, -1)])
    low, high = shift(own, GY, 1), shift(own, GY, -1)
    grads, back_low, back_own, back_high = work(low, own, high, goal, weights)
    mine, other = reduce_all(grads)
    wide = back_own + (shift(back_low, GY, -1) + shift(back_high, GY, 1))
    spread = restore(wide[1], shift(wide[0], GX, -1), shift(wide[2], GX, 1))
    loss, embed, norm, attend, output, second, expand, reduce, decode = finish(mine, other, lax.axis_index("co").reshape(1))
    field_back = loss[0, 1] * spread
    return loss[0, 0], field_back, embed, norm[0], attend, output, second[0], expand, reduce, decode


def solution(mesh):
    fine = Mesh(mesh.devices.reshape(16, 2, 4, 2, 2), AXES)
    block = P(GX, GY, None)
    in_specs = (block, block) + (P(),) * 8
    out_specs = (P(), block) + (P(),) * 8
    return jax.shard_map(shards, mesh=fine, in_specs=in_specs, out_specs=out_specs, check_vma=False)
```

time: 823 us -> 220 us (0.27)
  waiting for transfers between devices: 379 us -> 17.5 us
  local copies, waits for them, and re-layouts: 147 us -> 10.6 us
  matrix products: 67.6 us -> 0 us
  Pallas kernels: 0 us -> 54.9 us
  blocking collectives: 108 us -> 82.7 us
  other arithmetic: 26.2 us -> 3.73 us
  between operations: 20.3 us -> 0.84 us
  starting transfers between devices: 63 us -> 45.4 us
    psum x1 -> x0, waiting for transfers between devices: 361 us -> none  [shards(): summed = lax.psum(tuple(gradients), ('gx', 'gy'))]
    psum x1 -> x0, blocking collectives: 108 us -> none  [shards(): misfit = lax.psum(local_misfit, ('gx', 'gy'))]
    all_to_all x0 -> x4, blocking collectives: none -> 82.7 us  [swap(): return lax.all_to_all(x, axes, 0, 0, tiled=True)]
    dot_general x48 -> x0, matrix products: 67.6 us -> none  [the longest x36 49.2 us: matmul(): return jnp.dot(left, right, precision=EXACT)]
    pallas_call x0 -> x4, Pallas kernels: none -> 54.9 us  [the longest x1 47.9 us: work(): return call(main_kernel, outs, scratch, 'work')(low, own, high, goal, *args)]
    unnamed x462 -> x26, local copies, waits for them, and re-layouts: 58.7 us -> 5.9 us
    transpose x12 -> x0, local copies, waits for them, and re-layouts: 34.5 us -> none  [the longest x4 25.9 us: closure(): ext.reshape(across, PATCH, along, PATCH, 3, upward, PATCH)]
    reshape x16 -> x2, local copies, waits for them, and re-layouts: 29.9 us -> 0.03 us  [the longest x1 0.02 us: reduce_all(): swap(jnp.broadcast_to(total, (16,) + total.shape), 'z')]
  transfers between devices with their start and end apart: 17 -> 10, of which waited for: 8 -> 6; matrix products, arithmetic and copies ran while one was open for 1% -> 1% of each run, Pallas kernels for 0% -> 1%
where the time goes in v1:
time: 220 us; the launch traced here: 216 us
  blocking collectives  82.7 us (38%)
  Pallas kernels  54.9 us (25%)
  starting transfers between devices  45.4 us (21%)
  waiting for transfers between devices  17.5 us (8%)
  local copies, waits for them, and re-layouts  10.6 us (5%)
  other arithmetic  3.73 us (2%)
    all_to_all x4, blocking collectives, swap(): return lax.all_to_all(x, axes, 0, 0, tiled=True)  82.7 us
    pallas_call x1, Pallas kernels, work(): return call(main_kernel, outs, scratch, 'work')(low, own, high, goal, *args)  47.9 us
    ppermute x8, starting transfers between devices, shift(): lax.ppermute(x, axes, [(i, (i + step) % count) for i in range(count)])  36 us
    ppermute x8, waiting for transfers between devices, shift(): lax.ppermute(x, axes, [(i, (i + step) % count) for i in range(count)])  14.2 us
    ppermute x1, starting transfers between devices, reduce_all(): return (total, lax.ppermute(total, 'co', [(0, 1), (1, 0)]))  7.48 us
    unnamed x26, local copies, waits for them, and re-layouts  5.9 us
  transfers between devices with their start and end apart: 10, of which 6 were waited for; matrix products, arithmetic and copies ran while one was open for 1% of the time, Pallas kernels for 1%

profile of v1, /device:TPU:1, one launch (start us, length us, event | category | flops | bytes accessed | tf_op | source)
XLA Modules:
  0.0 215.7 jit_solution(6933305827942185313)
XLA Ops:
  0.6 1.8 prepare.1
  2.5 3.9 %collective-permute-start = (f32[64,256]{1,0:T(8,128)}, f32[64,256]{1,0:T(8,128)S(1)}, u32[]{:S(2)}, u32[]{:S(2)}) collective-permute-start(f32[64,256]{1,0:T(8,128)} %get-tuple-element.25), channel_id=1, source_target_pairs={{0,16},{16,32},{32,48},{48,64},{64,80},{80,96},{96,112},{112,128},... | collective-permute-start | bytes 196616 | tf_op jit(solution)/shard_map/ppermute | solution.py:468
  6.4 10.9 %collective-permute-start.1 = (f32[64,256]{1,0:T(8,128)}, f32[64,256]{1,0:T(8,128)S(1)}, u32[]{:S(2)}, u32[]{:S(2)}) collective-permute-start(f32[64,256]{1,0:T(8,128)} %get-tuple-element.25), channel_id=1, source_target_pairs={{0,496},{16,0},{32,16},{48,32},{64,48},{80,64},{96,80},{112,96},{1... | collective-permute-start | bytes 196616 | tf_op jit(solution)/shard_map/ppermute | solution.py:468
  17.3 0.0 collective-permute-done
  17.3 1.6 collective-permute-done.1
  18.9 0.9 pad_maximum_fusion.refs_1_
  19.7 0.0 copy-start.3
  19.8 5.8 %collective-permute-start.2 = (f32[3,64,256]{2,1,0:T(8,128)S(1)}, f32[3,64,256]{2,1,0:T(8,128)S(1)}, u32[]{:S(2)}, u32[]{:S(2)}) collective-permute-start(f32[3,64,256]{2,1,0:T(8,128)S(1)} %pad_maximum_fusion.refs_1_), channel_id=1, source_target_pairs={{0,1},{1,2},{2,3},{3,4},{4,5},{5,6},{6,7},{7,8},{8,9},{9,10},{10,1... | collective-permute-start | bytes 589832 | tf_op jit(solution)/shard_map/ppermute | solution.py:468
  25.5 1.9 collective-permute-start.3
  27.5 1.8 copy.22.refs_11_
  29.2 0.0 collective-permute-done.2.refs_0_
  29.2 0.0 copy-start.6
  29.2 4.8 %collective-permute-done.3.refs_2_ = f32[3,64,256]{2,1,0:T(8,128)S(1)} collective-permute-done((f32[3,64,256]{2,1,0:T(8,128)S(1)}, f32[3,64,256]{2,1,0:T(8,128)S(1)}, u32[]{:S(2)}, u32[]{:S(2)}) %collective-permute-start.3) | collective-permute-done | bytes 196640 | tf_op jit(solution)/shard_map/ppermute | solution.py:468
  34.0 0.0 copy-start.7
  34.0 0.0 copy-done.3
  34.0 0.0 copy-done.6
  34.0 0.7 copy-done.7
  34.7 47.9 %work.1 = (f32[2560,256]{1,0:T(8,128)}, f32[3,64,256]{2,1,0:T(8,128)}, f32[3,64,256]{2,1,0:T(8,128)}, f32[3,64,256]{2,1,0:T(8,128)}) custom-call(f32[3,64,256]{2,1,0:T(8,128)} %copy-done.6, f32[3,64,256]{2,1,0:T(8,128)} %copy-done.3, f32[3,64,256]{2,1,0:T(8,128)} %copy-done.7, f32[64,256]{1,0:T(8,128)} %get-tuple-element.26.refs_3_, f32[192,256]{1,0:T(8,128)} %refs_4_.1, ...), custom_call_target="tpu_custom_call" | custom-call | tf_op jit(solution)/shard_map/work/pallas_call | solution.py:444
  82.6 0.0 copy-start.1
  82.6 2.6 %dynamic-slice_bitcast_fusion = f32[1280,256]{1,0:T(8,128)} fusion(f32[2,1280,256]{2,1,0:T(8,128)} %bitcast.26, s32[]{:T(128)S(6)} %select_n.8), kind=kLoop, calls=%fused_computation.1 | loop fusion | bytes 2621444 | tf_op jit(solution)/shard_map/jit(dynamic_index_in_dim)/squeeze | solution.py:482
  85.2 1.9 collective-permute-start.4
  87.1 3.3 %collective-permute-done.4 = f32[1280,256]{1,0:T(8,128)} collective-permute-done((f32[1280,256]{1,0:T(8,128)}, f32[1280,256]{1,0:T(8,128)}, u32[]{:S(2)}, u32[]{:S(2)}) %collective-permute-start.4) | collective-permute-done | bytes 1310752 | tf_op jit(solution)/shard_map/ppermute | solution.py:483
  90.5 0.0 copy-done.1
  90.5 1.5 bitcast_add_fusion
  92.0 24.9 %all_to_all.20 = f32[16,80,256]{2,1,0:T(8,128)S(1)} all-to-all(f32[16,80,256]{2,1,0:T(8,128)S(1)} %bitcast.25), channel_id=1, replica_groups=mesh['z'=16,'xl'=2,'y'=4,'xh'=2,'co'=2] {'xl','y','xh'}, dimensions={0} | all-to-all | bytes 2621440 | tf_op jit(solution)/shard_map/all_to_all | solution.py:475
  116.9 0.1 reduce_sum.18
  117.0 21.8 %all_to_all.21 = f32[16,5,256]{2,1,0:T(8,128)S(1)} all-to-all(f32[16,5,256]{2,1,0:T(8,128)S(1)} %reshape.49), channel_id=1, replica_groups=mesh['z'=16,'xl'=2,'y'=4,'xh'=2,'co'=2] {'z'}, dimensions={0} | all-to-all | bytes 163840 | tf_op jit(solution)/shard_map/all_to_all | solution.py:475
  138.8 16.9 %all_to_all.22 = f32[16,5,256]{2,1,0:T(8,128)S(1)} all-to-all(f32[16,5,256]{2,1,0:T(8,128)S(1)} %broadcast_in_dim.6), channel_id=1, replica_groups=mesh['z'=16,'xl'=2,'y'=4,'xh'=2,'co'=2] {'z'}, dimensions={0} | all-to-all | bytes 163840 | tf_op jit(solution)/shard_map/all_to_all | solution.py:475
  155.7 0.1 broadcast_in_dim.7
  155.8 0.0 copy-start.11
  155.9 0.0 copy-start.10
  155.9 0.0 copy-start.5
  155.9 19.1 %all_to_all.23 = f32[16,80,256]{2,1,0:T(8,128)S(1)} all-to-all(f32[16,80,256]{2,1,0:T(8,128)S(1)} %broadcast_in_dim.7), channel_id=1, replica_groups=mesh['z'=16,'xl'=2,'y'=4,'xh'=2,'co'=2] {'xl','y','xh'}, dimensions={0} | all-to-all | bytes 2621440 | tf_op jit(solution)/shard_map/all_to_all | solution.py:475
  175.0 0.0 copy-start
  175.0 7.5 %collective-permute-start.5 = (f32[1280,256]{1,0:T(8,128)S(1)}, f32[1280,256]{1,0:T(8,128)S(1)}, u32[]{:S(2)}, u32[]{:S(2)}) collective-permute-start(f32[1280,256]{1,0:T(8,128)S(1)} %bitcast.23), channel_id=1, source_target_pairs={{0,1},{1,0},{2,3},{3,2},{4,5},{5,4},{6,7},{7,6},{8,9},{9,8},{10,11... | collective-permute-start | bytes 3932168 | tf_op jit(solution)/shard_map/ppermute | solution.py:488
  182.5 0.0 copy-done.11
  182.5 1.9 collective-permute-start.6
  184.4 0.0 copy-done.10
  184.4 5.1 %collective-permute-start.7 = (f32[3,64,256]{2,1,0:T(8,128)S(1)}, f32[3,64,256]{2,1,0:T(8,128)S(1)}, u32[]{:S(2)}, u32[]{:S(2)}) collective-permute-start(f32[3,64,256]{2,1,0:T(8,128)S(1)} %copy-done.10), channel_id=1, source_target_pairs={{0,1},{1,2},{2,3},{3,4},{4,5},{5,6},{6,7},{7,8},{8,9},{9,10},{10,1... | collective-permute-start | bytes 589832 | tf_op jit(solution)/shard_map/ppermute | solution.py:468
  189.6 1.4 collective-permute-done.6
  191.0 1.2 collective-permute-done.7
  192.2 0.0 copy-done.5
  192.2 0.6 slice_bitcast_fusion
  192.8 4.5 %collective-permute-start.8 = (f32[64,256]{1,0:T(8,128)S(1)}, f32[64,256]{1,0:T(8,128)S(1)}, u32[]{:S(2)}, u32[]{:S(2)}) collective-permute-start(f32[64,256]{1,0:T(8,128)S(1)} %get-tuple-element.61), channel_id=1, source_target_pairs={{0,496},{16,0},{32,16},{48,32},{64,48},{80,64},{96,80},{112,96},{1... | collective-permute-start | bytes 196616 | tf_op jit(solution)/shard_map/ppermute | solution.py:468
  197.4 1.9 collective-permute-start.9
  199.3 0.0 collective-permute-done.8.b_ref
  199.3 0.0 copy-start.8
  199.3 5.2 %collective-permute-done.9.c_ref = f32[64,256]{1,0:T(8,128)S(1)} collective-permute-done((f32[64,256]{1,0:T(8,128)S(1)}, f32[64,256]{1,0:T(8,128)S(1)}, u32[]{:S(2)}, u32[]{:S(2)}) %collective-permute-start.9) | collective-permute-done | bytes 65568 | tf_op jit(solution)/shard_map/ppermute | solution.py:468
  204.5 0.0 copy-start.9
  204.5 0.0 copy-done.8
  204.5 0.6 copy-done.9
  205.1 1.8 restore.1
  206.9 0.0 collective-permute-done.5.other
  206.9 0.0 copy-start.2
  206.9 0.0 copy-done
  206.9 1.1 copy-done.2
  207.9 0.0 copy-start.4
  207.9 3.4 %finish.1 = (f32[1,128]{1,0:T(1,128)}, f32[192,256]{1,0:T(8,128)}, f32[1,256]{1,0:T(1,128)}, f32[256,768]{1,0:T(8,128)}, f32[256,256]{1,0:T(8,128)}, /*index=5*/...) custom-call(s32[1]{0:T(128)} %bitcast.core, f32[1280,256]{1,0:T(8,128)} %bitcast.24, ...), custom_call_target="tpu_custom_call" | custom-call | tf_op jit(solution)/shard_map/finish/pallas_call | solution.py:459
  211.3 1.3 fusion
  212.7 1.7 copy.23
  214.4 0.0 copy-done.4
  214.4 1.3 broadcast_multiply_fusion
  (5 shorter events, 0.1 us)
Async XLA Ops:
  2.5 14.8 %collective-permute-start = (f32[64,256]{1,0:T(8,128)}, f32[64,256]{1,0:T(8,128)S(1)}, u32[]{:S(2)}, u32[]{:S(2)}) collective-permute-start(f32[64,256]{1,0:T(8,128)} %get-tuple-element.25), channel_id=1, source_target_pairs={{0,16},{16,32},{32,48},{48,64},{64,80},{80,96},{96,112},{112,128},... | collective-permute-start | bytes 196616 | tf_op jit(solution)/shard_map/ppermute | solution.py:468
  6.4 12.5 %collective-permute-start.1 = (f32[64,256]{1,0:T(8,128)}, f32[64,256]{1,0:T(8,128)S(1)}, u32[]{:S(2)}, u32[]{:S(2)}) collective-permute-start(f32[64,256]{1,0:T(8,128)} %get-tuple-element.25), channel_id=1, source_target_pairs={{0,496},{16,0},{32,16},{48,32},{64,48},{80,64},{96,80},{112,96},{1... | collective-permute-start | bytes 196616 | tf_op jit(solution)/shard_map/ppermute | solution.py:468
  19.7 14.3 %copy-start.3 = (f32[3,64,256]{2,1,0:T(8,128)}, f32[3,64,256]{2,1,0:T(8,128)S(1)}, u32[]{:S(2)}) copy-start(f32[3,64,256]{2,1,0:T(8,128)S(1)} %pad_maximum_fusion.refs_1_) | copy-start | bytes 589828
  19.8 9.5 %collective-permute-start.2 = (f32[3,64,256]{2,1,0:T(8,128)S(1)}, f32[3,64,256]{2,1,0:T(8,128)S(1)}, u32[]{:S(2)}, u32[]{:S(2)}) collective-permute-start(f32[3,64,256]{2,1,0:T(8,128)S(1)} %pad_maximum_fusion.refs_1_), channel_id=1, source_target_pairs={{0,1},{1,2},{2,3},{3,4},{4,5},{5,6},{6,7},{7,8},{8,9},{9,10},{10,1... | collective-permute-start | bytes 589832 | tf_op jit(solution)/shard_map/ppermute | solution.py:468
  25.5 8.5 %collective-permute-start.3 = (f32[3,64,256]{2,1,0:T(8,128)S(1)}, f32[3,64,256]{2,1,0:T(8,128)S(1)}, u32[]{:S(2)}, u32[]{:S(2)}) collective-permute-start(f32[3,64,256]{2,1,0:T(8,128)S(1)} %pad_maximum_fusion.refs_1_), channel_id=1, source_target_pairs={{0,15},{1,0},{2,1},{3,2},{4,3},{5,4},{6,5},{7,6},{8,7},{9,8},{10,9... | collective-permute-start | bytes 589832 | tf_op jit(solution)/shard_map/ppermute | solution.py:468
  29.2 4.8 %copy-start.6 = (f32[3,64,256]{2,1,0:T(8,128)}, f32[3,64,256]{2,1,0:T(8,128)S(1)}, u32[]{:S(2)}) copy-start(f32[3,64,256]{2,1,0:T(8,128)S(1)} %collective-permute-done.2.refs_0_) | copy-start | bytes 589828
  34.0 0.7 copy-start.7
  82.6 7.9 %copy-start.1 = (f32[2560,256]{1,0:T(8,128)S(1)}, f32[2560,256]{1,0:T(8,128)}, u32[]{:S(2)}) copy-start(f32[2560,256]{1,0:T(8,128)} %get-tuple-element.27) | copy-start | bytes 7864324
  85.2 5.3 %collective-permute-start.4 = (f32[1280,256]{1,0:T(8,128)}, f32[1280,256]{1,0:T(8,128)}, u32[]{:S(2)}, u32[]{:S(2)}) collective-permute-start(f32[1280,256]{1,0:T(8,128)} %dynamic-slice_bitcast_fusion), channel_id=1, source_target_pairs={{0,1},{1,0},{2,3},{3,2},{4,5},{5,4},{6,7},{7,6},{8,9},{9,8},{10,11... | collective-permute-start | bytes 3932168 | tf_op jit(solution)/shard_map/ppermute | solution.py:483
  155.8 26.6 %copy-start.11 = (f32[3,64,256]{2,1,0:T(8,128)S(1)}, f32[3,64,256]{2,1,0:T(8,128)}, u32[]{:S(2)}) copy-start(f32[3,64,256]{2,1,0:T(8,128)} %get-tuple-element.30) | copy-start | bytes 589828
  155.9 28.5 %copy-start.10 = (f32[3,64,256]{2,1,0:T(8,128)S(1)}, f32[3,64,256]{2,1,0:T(8,128)}, u32[]{:S(2)}) copy-start(f32[3,64,256]{2,1,0:T(8,128)} %get-tuple-element.31) | copy-start | bytes 589828
  155.9 36.3 %copy-start.5 = (f32[3,64,256]{2,1,0:T(8,128)S(1)}, f32[3,64,256]{2,1,0:T(8,128)}, u32[]{:S(2)}) copy-start(f32[3,64,256]{2,1,0:T(8,128)} %get-tuple-element.29) | copy-start | bytes 589828
  175.0 31.9 %copy-start = (f32[16,80,256]{2,1,0:T(8,128)}, f32[16,80,256]{2,1,0:T(8,128)S(1)}, u32[]{:S(2)}) copy-start(f32[16,80,256]{2,1,0:T(8,128)S(1)} %all_to_all.23) | copy-start | bytes 3932164
  175.0 31.9 %collective-permute-start.5 = (f32[1280,256]{1,0:T(8,128)S(1)}, f32[1280,256]{1,0:T(8,128)S(1)}, u32[]{:S(2)}, u32[]{:S(2)}) collective-permute-start(f32[1280,256]{1,0:T(8,128)S(1)} %bitcast.23), channel_id=1, source_target_pairs={{0,1},{1,0},{2,3},{3,2},{4,5},{5,4},{6,7},{7,6},{8,9},{9,8},{10,11... | collective-permute-start | bytes 3932168 | tf_op jit(solution)/shard_map/ppermute | solution.py:488
  182.5 8.5 %collective-permute-start.6 = (f32[3,64,256]{2,1,0:T(8,128)S(1)}, f32[3,64,256]{2,1,0:T(8,128)S(1)}, u32[]{:S(2)}, u32[]{:S(2)}) collective-permute-start(f32[3,64,256]{2,1,0:T(8,128)S(1)} %copy-done.11), channel_id=1, source_target_pairs={{0,15},{1,0},{2,1},{3,2},{4,3},{5,4},{6,5},{7,6},{8,7},{9,8},{10,9... | collective-permute-start | bytes 589832 | tf_op jit(solution)/shard_map/ppermute | solution.py:468
  184.4 7.7 %collective-permute-start.7 = (f32[3,64,256]{2,1,0:T(8,128)S(1)}, f32[3,64,256]{2,1,0:T(8,128)S(1)}, u32[]{:S(2)}, u32[]{:S(2)}) collective-permute-start(f32[3,64,256]{2,1,0:T(8,128)S(1)} %copy-done.10), channel_id=1, source_target_pairs={{0,1},{1,2},{2,3},{3,4},{4,5},{5,6},{6,7},{7,8},{8,9},{9,10},{10,1... | collective-permute-start | bytes 589832 | tf_op jit(solution)/shard_map/ppermute | solution.py:468
  192.8 6.5 %collective-permute-start.8 = (f32[64,256]{1,0:T(8,128)S(1)}, f32[64,256]{1,0:T(8,128)S(1)}, u32[]{:S(2)}, u32[]{:S(2)}) collective-permute-start(f32[64,256]{1,0:T(8,128)S(1)} %get-tuple-element.61), channel_id=1, source_target_pairs={{0,496},{16,0},{32,16},{48,32},{64,48},{80,64},{96,80},{112,96},{1... | collective-permute-start | bytes 196616 | tf_op jit(solution)/shard_map/ppermute | solution.py:468
  197.4 7.1 %collective-permute-start.9 = (f32[64,256]{1,0:T(8,128)S(1)}, f32[64,256]{1,0:T(8,128)S(1)}, u32[]{:S(2)}, u32[]{:S(2)}) collective-permute-start(f32[64,256]{1,0:T(8,128)S(1)} %get-tuple-element.60), channel_id=1, source_target_pairs={{0,16},{16,32},{32,48},{48,64},{64,80},{80,96},{96,112},{112,128},... | collective-permute-start | bytes 196616 | tf_op jit(solution)/shard_map/ppermute | solution.py:468
  199.3 5.2 %copy-start.8 = (f32[64,256]{1,0:T(8,128)}, f32[64,256]{1,0:T(8,128)S(1)}, u32[]{:S(2)}) copy-start(f32[64,256]{1,0:T(8,128)S(1)} %collective-permute-done.8.b_ref) | copy-start | bytes 196612
  204.5 0.6 copy-start.9
  206.9 1.1 copy-start.2
  207.9 6.5 %copy-start.4 = (f32[8,8,192]{2,1,0:T(8,128)S(1)}, f32[8,8,192]{2,1,0:T(8,128)}, u32[]{:S(2)}) copy-start(f32[8,8,192]{2,1,0:T(8,128)} %restore.1) | copy-start | bytes 147460

commit v2 on v1

--- a/solution.py
+++ b/solution.py
@@ -68,8 +68,7 @@
     to_tokens(target_ref, rows_ref, turned_ref, goal_ref)
 
 
-def restore_kernel(a_ref, b_ref, c_ref, out_ref, turned_ref, rows_ref):
-    total = a_ref[...] + (b_ref[...] + c_ref[...])
+def from_tokens(total, out_ref, turned_ref, rows_ref):
     lane = lanes((16, 128))
     for c in range(3):
         for dz in range(4):
@@ -92,7 +91,6 @@
 
 
 def inner_rows(ref, m, n, dx=0, dy=0):
-    width = ref.shape[1]
     parts = [ref[((X + 1 + dx) * m + 1 + dy) * 16 : ((X + 1 + dx) * m + 1 + dy + n) * 16, :] for X in range(n)]
     return jnp.concatenate(parts, axis=0)
 
@@ -187,28 +185,41 @@
     return row // 16 == lanes((128, 256)) // 32
 
 
+def pair_mask():
+    key = lax.broadcasted_iota(jnp.int32, (192, 256), 0) // 16 % 4
+    query = lanes((192, 256)) // 128
+    return (key >= query) & (key < query + 3)
+
+
 def by_head(x, mask):
-    wide = jnp.where(mask, jnp.concatenate([x] * 8, axis=0), 0.0)
-    return split(wide)
+    wide = [jnp.where(mask, jnp.concatenate([x[k * 16 : k * 16 + 16]] * 8, axis=0), 0.0) for k in range(2)]
+    return split(jnp.concatenate(wide, axis=0))
 
 
 def from_heads(x, mask):
-    kept = jnp.where(mask, x, 0.0)
-    total = kept[0:16]
-    for head in range(1, 8):
-        total = total + kept[head * 16 : head * 16 + 16]
-    return total
+    columns = []
+    for k in range(2):
+        kept = jnp.where(mask, x[128 * k : 128 * k + 128], 0.0)
+        total = [kept[head * 16 : head * 16 + 16] for head in range(8)]
+        while len(total) > 1:
+            total = [total[i] + total[i + 1] for i in range(0, len(total), 2)]
+        columns.append(total[0])
+    return jnp.concatenate(columns, axis=0)
 
 
 def key_rows(X, Y, m):
-    return [pl.multiple_of(((X + dx) * m + Y) * 16, 16) for dx in range(3)]
+    return [((X + dx) * m + Y) * 16 for dx in range(3)]
 
 
 def gather(ref, starts, low, high):
     def one(which):
-        return jnp.concatenate([ref[which, pl.ds(s, 48), low:high] for s in starts], axis=0)
+        return jnp.concatenate([ref[which, s : s + 64, low:high] for s in starts], axis=0)
 
     return one(0), one(1)
+
+
+def pairs_of(n):
+    return [(X, Y) for X in range(n) for Y in range(0, n, 2)]
 
 
 def forward(w, g1, g2, ext_ref, r, m, n, chunk):
@@ -228,19 +239,21 @@
     q[...] = dot(normed_in, (w["attend"][0, :, :256], w["attend"][1, :, :256]))
     mask = head_mask()
 
-    def attend(i, _):
-        X, Y = i // n, i % n
-        starts = key_rows(X, Y, m)
-        here = pl.multiple_of(i * 16, 16)
-        wide = by_head(q[pl.ds(here, 16), :], mask)
-        scores = dot(gather(kv, starts, 0, 256), wide, 1, 1)
-        weights = jnp.exp(scores * FACTOR)
-        weights = weights / jnp.sum(weights, axis=0, keepdims=True)
-        wts[i] = weights
-        att[pl.ds(here, 16), :] = from_heads(dot(split(weights), gather(kv, starts, 256, 512), 0, 0), mask)
-        return 0
-
-    lax.fori_loop(0, n * n, attend, 0)
+    allowed = pair_mask()
+
+    def attend(pairs):
+        results = []
+        for X, Y in pairs:
+            starts = key_rows(X, Y, m)
+            wide = by_head(q[(X * n + Y) * 16 : (X * n + Y) * 16 + 32, :], mask)
+            weights = jnp.where(allowed, jnp.exp(dot(gather(kv, starts, 0, 256), wide, 1, 1) * FACTOR), 0.0)
+            weights = weights / jnp.sum(weights, axis=0, keepdims=True)
+            results.append((weights, from_heads(dot(split(weights), gather(kv, starts, 256, 512), 0, 0), mask)))
+        for (X, Y), (weights, attended) in zip(pairs, results):
+            wts[X * (n // 2) + Y // 2] = weights
+            att[(X * n + Y) * 16 : (X * n + Y) * 16 + 32, :] = attended
+
+    attend(pairs_of(n))
     middle = inner_rows(tok, m, n) + dot(split(att[...]), both(w["output"]))
     mid[...] = middle
     hidden = dot(split(middle * rms(middle) * g2), both(w["expand"]))
@@ -274,7 +287,7 @@
     return jnp.concatenate(halves, axis=1)
 
 
-def backward(w, g1, g2, ext_ref, back_ref, grads, r, dkv, dq, g, m, n, chunk, first):
+def backward(w, g1, g2, ext_ref, back_ref, grads, r, dkv, dq, g, m, n, first):
     (tok, nrm, kv, q, wts, att, mid, h, late) = r
     dclosure = split(0.1 * g)
     add_rows(grads, DECODE, dot(dclosure, split(late[...]), 0, 0)[:192], first)
@@ -298,25 +311,25 @@
     dkv[...] = jnp.zeros(dkv.shape, F32)
     mask = head_mask()
 
-    def attend(i, _):
-        X, Y = i // n, i % n
-        starts = key_rows(X, Y, m)
-        here = pl.multiple_of(i * 16, 16)
-        wide = by_head(q[pl.ds(here, 16), :], mask)
-        dwide = by_head(att[pl.ds(here, 16), :], mask)
-        weights = wts[i]
-        dweights = dot(gather(kv, starts, 256, 512), dwide, 1, 1)
-        common = jnp.sum(weights * dweights, axis=0, keepdims=True)
-        dscores = split(weights * (dweights - common) * FACTOR)
-        dq[pl.ds(here, 16), :] = from_heads(dot(dscores, gather(kv, starts, 0, 256), 0, 0), mask)
-        dkeys = dot(dscores, wide)
-        dvals = dot(split(weights), dwide)
-        for k, s in enumerate(starts):
-            dkv[pl.ds(s, 48), 0:256] += dkeys[k * 48 : k * 48 + 48]
-            dkv[pl.ds(s, 48), 256:512] += dvals[k * 48 : k * 48 + 48]
-        return 0
-
-    lax.fori_loop(0, n * n, attend, 0)
+    def attend(pairs):
+        results = []
+        for X, Y in pairs:
+            starts = key_rows(X, Y, m)
+            here = slice((X * n + Y) * 16, (X * n + Y) * 16 + 32)
+            wide, dwide = by_head(q[here, :], mask), by_head(att[here, :], mask)
+            weights = wts[X * (n // 2) + Y // 2]
+            dweights = dot(gather(kv, starts, 256, 512), dwide, 1, 1)
+            common = jnp.sum(weights * dweights, axis=0, keepdims=True)
+            dscores = split(weights * (dweights - common) * FACTOR)
+            dqueries = from_heads(dot(dscores, gather(kv, starts, 0, 256), 0, 0), mask)
+            results.append((dqueries, dot(dscores, wide), dot(split(weights), dwide)))
+        for (X, Y), (dqueries, dkeys, dvals) in zip(pairs, results):
+            dq[(X * n + Y) * 16 : (X * n + Y) * 16 + 32, :] = dqueries
+            for k, s in enumerate(key_rows(X, Y, m)):
+                dkv[s : s + 64, 0:256] += dkeys[k * 64 : k * 64 + 64]
+                dkv[s : s + 64, 256:512] += dvals[k * 64 : k * 64 + 64]
+
+    attend(pairs_of(n))
     normed_in = inner_rows(nrm.at[0], m, n), inner_rows(nrm.at[1], m, n)
     dquery = split(dq[...])
     add_rows(grads, ATTEND, dot(normed_in, dquery, 0, 0), first)
@@ -343,9 +356,10 @@
 
 
 def main_kernel(*refs):
-    (low, own, high, goal, embed, gain1, attend, output, gain2, expand, reduce, decode) = refs[:12]
-    (grads, out_low, out_own, out_high) = refs[12:16]
-    scratch = list(refs[16:])
+    (core, low, own, high, goal, embed, gain1, attend, output, gain2, expand, reduce, decode) = refs[:13]
+    (kept, sent, out_low, out_own, out_high) = refs[13:18]
+    scratch = list(refs[18:])
+    grads = scratch.pop(0)
     w = {}
     for name in ("embed", "attend", "output", "expand", "reduce", "decode"):
         w[name] = scratch.pop(0)
@@ -353,7 +367,7 @@
     ext0, back0, ext1, back1, dkv0, dkv1, dq0, dq1 = scratch[:8]
     r0, r1 = scratch[8:17], scratch[17:26]
     put(w["embed"], 0, reorder(strip, embed[...]))
-    put(w["decode"], 0, reorder(strip, decode[...].T))
+    put(w["decode"], 0, reorder(strip, decode[...]))
     put(w["embed"], 192, jnp.zeros((64, 256), F32))
     put(w["decode"], 192, jnp.zeros((64, 256), F32))
     put(w["attend"], 0, attend[...])
@@ -361,11 +375,11 @@
     put(w["expand"], 0, expand[...])
     put(w["reduce"], 0, reduce[...])
     g1, g2 = gain1[...], gain2[...]
-    places = [
+    spots = [
         (by, bx, (px * 2 + py) * 16, ((2 * bx + px) * 6 + 2 * by + py) * 16)
         for by in range(3) for bx in range(3) for px in range(2) for py in range(2)
     ]
-    for by, bx, source, place in places:
+    for by, bx, source, place in spots:
         ext0[place : place + 16, :] = (low, own, high)[by][bx, source : source + 16, :]
     ext1[...] = stencil(ext0, 6, 4) + 0.1 * forward(w, g1, g2, ext0, r0, 6, 4, 192)
     final = stencil(ext1, 4, 2) + 0.1 * forward(w, g1, g2, ext1, r1, 4, 2, 128)
@@ -374,20 +388,27 @@
     sums = [jnp.sum(jnp.sum(v * v, axis=0, keepdims=True), axis=1, keepdims=True) for v in (residue, goal[...])]
     lane = lanes((1, 256))
     grads[SMALL + 2 : SMALL + 3, :] = jnp.where(lane == 0, sums[0], jnp.where(lane == 1, sums[1], 0.0))
-    backward(w, g1, g2, ext1, back1, grads, r1, dkv1, dq1, 2.0 * residue, 4, 2, 128, True)
-    backward(w, g1, g2, ext0, back0, grads, r0, dkv0, dq0, back1[...], 6, 4, 192, False)
-    for by, bx, source, place in places:
+    backward(w, g1, g2, ext1, back1, grads, r1, dkv1, dq1, 2.0 * residue, 4, 2, True)
+    backward(w, g1, g2, ext0, back0, grads, r0, dkv0, dq0, back1[...], 6, 4, False)
+    for by, bx, source, place in spots:
         (out_low, out_own, out_high)[by][bx, source : source + 16, :] = back0[place : place + 16, :]
-
-
-def finish_kernel(core, mine, other, loss, embed, norm, attend, output, second, expand, reduce, decode, strip, red):
+    half = ROWS // 2
+    kept[...] = grads[pl.ds(pl.multiple_of(core[0] * half, half), half), :]
+    sent[...] = grads[pl.ds(pl.multiple_of((1 - core[0]) * half, half), half), :]
+
+
+def finish_kernel(
+    core, mine, other, wide, before, after,
+    loss, field, embed, norm, attend, output, second, expand, reduce, decode, strip, red, turned, rows,
+):
     first = core[0] == 0
     red[0 : ROWS // 2, :] = jnp.where(first, mine[...], other[...])
     red[ROWS // 2 :, :] = jnp.where(first, other[...], mine[...])
     misfit = red[SMALL + 2 : SMALL + 3, 0:1]
     energy = red[SMALL + 2 : SMALL + 3, 1:2]
     scale = 6291456.0 / energy
-    loss[...] = jnp.where(lanes((1, 128)) == 0, misfit / energy, scale)
+    loss[...] = misfit / energy
+    from_tokens(scale * (wide[1] + (before[...] + after[...])), field, turned, rows)
     embed[...] = scale * reorder(strip, red[EMBED:ATTEND, :], True)
     for k in range(3):
         attend[:, 256 * k : 256 * k + 256] = scale * red[ATTEND + 256 * k : ATTEND + 256 * k + 256, :]
@@ -395,22 +416,25 @@
     for k in range(2):
         expand[:, 256 * k : 256 * k + 256] = scale * red[EXPAND + 256 * k : EXPAND + 256 * k + 256, :]
     reduce[...] = scale * red[REDUCE:DECODE, :]
-    decode[...] = (scale * reorder(strip, red[DECODE:SMALL, :], True)).T
+    decode[...] = scale * reorder(strip, red[DECODE:SMALL, :], True)
     norm[...] = scale * red[SMALL : SMALL + 1, :]
     second[...] = scale * red[SMALL + 1 : SMALL + 2, :]
 
 
+def places(scalars, arrays):
+    return [pl.BlockSpec(memory_space=pltpu.SMEM)] * scalars + [pl.BlockSpec(memory_space=pltpu.VMEM)] * arrays
+
+
 def arr(*shape, dtype=F32):
     return jax.ShapeDtypeStruct(shape, dtype)
 
 
-def call(kernel, outs, scratch, name, **more):
+def call(kernel, outs, scratch, **more):
     return pl.pallas_call(
         kernel,
         out_shape=outs,
         scratch_shapes=scratch,
         compiler_params=pltpu.CompilerParams(vmem_limit_bytes=VMEM_LIMIT),
-        name=name,
         interpret=INTERPRET,
         **more,
     )
@@ -418,45 +442,43 @@
 
 def prepare(field, target):
     scratch = [pltpu.VMEM((64, 192), F32), pltpu.VMEM((192, 128), F32)]
-    return call(prepare_kernel, (arr(64, 256), arr(64, 256)), scratch, "prepare")(field, target)
-
-
-def work(low, own, high, goal, weights):
+    return call(prepare_kernel, (arr(64, 256), arr(64, 256)), scratch)(field, target)
+
+
+def work(core, low, own, high, goal, weights):
     def V(*shape, dtype=F32):
         return pltpu.VMEM(shape, dtype)
 
     def kept(te, ti, n):
         return [
-            V(te, 256), V(2, te, 256, dtype=BF16), V(2, te, 512, dtype=BF16), V(ti, 256), V(n * n, 144, 128),
+            V(te, 256), V(2, te, 256, dtype=BF16), V(2, te, 512, dtype=BF16), V(ti, 256), V(n * n // 2, 192, 256),
             V(ti, 256), V(ti, 256), V(ti, 512), V(ti, 256),
         ]
 
     scratch = [
-        V(2, 256, 256, dtype=BF16), V(2, 256, 768, dtype=BF16), V(2, 256, 256, dtype=BF16),
+        V(ROWS, 256), V(2, 256, 256, dtype=BF16), V(2, 256, 768, dtype=BF16), V(2, 256, 256, dtype=BF16),
         V(2, 256, 512, dtype=BF16), V(2, 512, 256, dtype=BF16), V(2, 256, 256, dtype=BF16),
         V(2, 192, 128),
         V(576, 256), V(576, 256), V(256, 256), V(256, 256), V(576, 512), V(256, 512), V(256, 256), V(64, 256),
         *kept(576, 256, 4), *kept(256, 64, 2),
     ]
-    outs = (arr(ROWS, 256), arr(3, 64, 256), arr(3, 64, 256), arr(3, 64, 256))
+    half = arr(ROWS // 2, 256)
+    outs = (half, half, arr(3, 64, 256), arr(3, 64, 256), arr(3, 64, 256))
     embed, gain1, attend, output, gain2, expand, reduce, decode = weights
-    args = (embed, gain1.reshape(1, 256), attend, output, gain2.reshape(1, 256), expand, reduce, decode)
-    return call(main_kernel, outs, scratch, "work")(low, own, high, goal, *args)
-
-
-def restore(a, b, c):
-    scratch = [pltpu.VMEM((192, 128), F32), pltpu.VMEM((128, 192), F32)]
-    return call(restore_kernel, arr(8, 8, 192), scratch, "restore")(a, b, c)
-
-
-def finish(mine, other, core):
+    args = (embed, gain1.reshape(1, 256), attend, output, gain2.reshape(1, 256), expand, reduce, decode.T)
+    return call(main_kernel, outs, scratch, in_specs=places(1, 12))(core, low, own, high, goal, *args)
+
+
+def finish(core, mine, other, wide, before, after):
     outs = (
-        arr(1, 128), arr(192, 256), arr(1, 256), arr(256, 768), arr(256, 256), arr(1, 256), arr(256, 512),
-        arr(512, 256), arr(256, 192),
+        arr(1, 1), arr(8, 8, 192), arr(192, 256), arr(1, 256), arr(256, 768), arr(256, 256), arr(1, 256),
+        arr(256, 512), arr(512, 256), arr(192, 256),
     )
-    scratch = [pltpu.VMEM((2, 192, 128), F32), pltpu.VMEM((ROWS, 256), F32)]
-    specs = [pl.BlockSpec(memory_space=pltpu.SMEM)] + [pl.BlockSpec(memory_space=pltpu.VMEM)] * 2
-    return call(finish_kernel, outs, scratch, "finish", in_specs=specs)(core, mine, other)
+    scratch = [
+        pltpu.VMEM((2, 192, 128), F32), pltpu.VMEM((ROWS, 256), F32),
+        pltpu.VMEM((192, 128), F32), pltpu.VMEM((128, 192), F32),
+    ]
+    return call(finish_kernel, outs, scratch, in_specs=places(1, 5))(core, mine, other, wide, before, after)
 
 
 AXES = ("z", "xl", "y", "xh", "co")
@@ -475,30 +497,26 @@
     return lax.all_to_all(x, axes, 0, 0, tiled=True)
 
 
-def reduce_all(grads):
-    core = lax.axis_index("co")
-    halves = grads.reshape(2, ROWS // 2, 256)
-    kept = lax.dynamic_index_in_dim(halves, core, 0, keepdims=False)
-    sent = lax.dynamic_index_in_dim(halves, 1 - core, 0, keepdims=False)
-    total = kept + lax.ppermute(sent, "co", [(0, 1), (1, 0)])
-    total = jnp.sum(swap(total.reshape(16, ROWS // 32, 256), PLANE), axis=0)
-    total = jnp.sum(swap(total.reshape(16, ROWS // 512, 256), "z"), axis=0)
-    total = swap(jnp.broadcast_to(total, (16,) + total.shape), "z").reshape(ROWS // 32, 256)
-    total = swap(jnp.broadcast_to(total, (16,) + total.shape), PLANE).reshape(ROWS // 2, 256)
-    return total, lax.ppermute(total, "co", [(0, 1), (1, 0)])
-
-
 def shards(field, target, *weights):
+    core = lax.axis_index("co").reshape(1)
+    half = ROWS // 2
+    swapped = [(0, 1), (1, 0)]
     tokens, goal = prepare(field, target)
     own = jnp.stack([shift(tokens, GX, 1), tokens, shift(tokens, GX, -1)])
     low, high = shift(own, GY, 1), shift(own, GY, -1)
-    grads, back_low, back_own, back_high = work(low, own, high, goal, weights)
-    mine, other = reduce_all(grads)
-    wide = back_own + (shift(back_low, GY, -1) + shift(back_high, GY, 1))
-    spread = restore(wide[1], shift(wide[0], GX, -1), shift(wide[2], GX, 1))
-    loss, embed, norm, attend, output, second, expand, reduce, decode = finish(mine, other, lax.axis_index("co").reshape(1))
-    field_back = loss[0, 1] * spread
-    return loss[0, 0], field_back, embed, norm[0], attend, output, second[0], expand, reduce, decode
+    kept, sent, back_low, back_own, back_high = work(core, low, own, high, goal, weights)
+    total = kept + lax.ppermute(sent, "co", swapped)
+    back_low, back_high = shift(back_low, GY, -1), shift(back_high, GY, 1)
+    wide = back_own + (back_low + back_high)
+    total = jnp.sum(swap(total.reshape(16, half // 16, 256), PLANE), axis=0)
+    before, after = shift(wide[0], GX, -1), shift(wide[2], GX, 1)
+    total = jnp.sum(swap(total.reshape(16, half // 256, 256), "z"), axis=0)
+    total = swap(jnp.broadcast_to(total, (16,) + total.shape), "z").reshape(half // 16, 256)
+    total = swap(jnp.broadcast_to(total, (16,) + total.shape), PLANE).reshape(half, 256)
+    other = lax.ppermute(total, "co", swapped)
+    results = finish(core, total, other, wide, before, after)
+    loss, field_back, embed, norm, attend, output, second, expand, reduce, decode = results
+    return loss[0, 0], field_back, embed, norm[0], attend, output, second[0], expand, reduce, decode.T
 
 
 def solution(mesh):

time: 220 us -> 191 us (0.87)
  the two profiles are of different devices: /device:TPU:1 before, /device:TPU:2 now
where the time goes in v2:
time: 191 us; the launch traced here: 190 us
  blocking collectives  83.1 us (44%)
  Pallas kernels  36.2 us (19%)
  waiting for transfers between devices  32.7 us (17%)
  starting transfers between devices  32.2 us (17%)
  local copies, waits for them, and re-layouts  2.54 us (1%)
  other arithmetic  2.48 us (1%)
    all_to_all x4, blocking collectives, swap(): return lax.all_to_all(x, axes, 0, 0, tiled=True)  83.1 us
    pallas_call x1, Pallas kernels, work(): call(main_kernel, outs, scratch, in_specs=places(1, 12))  31.1 us
    ppermute x8, waiting for transfers between devices, shift(): lax.ppermute(x, axes, [(i, (i + step) % count) for i in range(count)])  29.5 us
    ppermute x8, starting transfers between devices, shift(): lax.ppermute(x, axes, [(i, (i + step) % count) for i in range(count)])  28.4 us
  transfers between devices with their start and end apart: 10, of which 9 were waited for; matrix products, arithmetic and copies ran while one was open for 0% of the time, Pallas kernels for 0%

profile of v2, /device:TPU:2, one launch (start us, length us, event | category | flops | bytes accessed | tf_op | source)
XLA Modules:
  0.0 190.3 jit_solution(4221255405141867298)
XLA Ops:
  0.6 1.8 shard_map.177
  2.5 7.8 %collective-permute-start.1 = (f32[64,256]{1,0:T(8,128)}, f32[64,256]{1,0:T(8,128)S(1)}, u32[]{:S(2)}, u32[]{:S(2)}) collective-permute-start(f32[64,256]{1,0:T(8,128)} %get-tuple-element.27), channel_id=1, source_target_pairs={{0,496},{16,0},{32,16},{48,32},{64,48},{80,64},{96,80},{112,96},{1... | collective-permute-start | bytes 196616 | tf_op jit(solution)/shard_map/ppermute | solution.py:490
  10.3 1.9 %collective-permute-start = (f32[64,256]{1,0:T(8,128)}, f32[64,256]{1,0:T(8,128)S(1)}, u32[]{:S(2)}, u32[]{:S(2)}) collective-permute-start(f32[64,256]{1,0:T(8,128)} %get-tuple-element.27), channel_id=1, source_target_pairs={{0,16},{16,32},{32,48},{48,64},{64,80},{80,96},{96,112},{112,128},... | collective-permute-start | bytes 196616 | tf_op jit(solution)/shard_map/ppermute | solution.py:490
  12.2 0.3 collective-permute-done.1
  12.5 7.2 %collective-permute-done = f32[64,256]{1,0:T(8,128)S(1)} collective-permute-done((f32[64,256]{1,0:T(8,128)}, f32[64,256]{1,0:T(8,128)S(1)}, u32[]{:S(2)}, u32[]{:S(2)}) %collective-permute-start) | collective-permute-done | bytes 65568 | tf_op jit(solution)/shard_map/ppermute | solution.py:490
  19.7 0.9 pad_maximum_fusion.refs_2_
  20.5 0.0 copy-start.3
  20.6 4.8 %collective-permute-start.3 = (f32[3,64,256]{2,1,0:T(8,128)S(1)}, f32[3,64,256]{2,1,0:T(8,128)S(1)}, u32[]{:S(2)}, u32[]{:S(2)}) collective-permute-start(f32[3,64,256]{2,1,0:T(8,128)S(1)} %pad_maximum_fusion.refs_2_), channel_id=1, source_target_pairs={{0,15},{1,0},{2,1},{3,2},{4,3},{5,4},{6,5},{7,6},{8,7},{9,8},{10,9... | collective-permute-start | bytes 589832 | tf_op jit(solution)/shard_map/ppermute | solution.py:490
  25.3 1.9 %collective-permute-start.2 = (f32[3,64,256]{2,1,0:T(8,128)S(1)}, f32[3,64,256]{2,1,0:T(8,128)S(1)}, u32[]{:S(2)}, u32[]{:S(2)}) collective-permute-start(f32[3,64,256]{2,1,0:T(8,128)S(1)} %pad_maximum_fusion.refs_2_), channel_id=1, source_target_pairs={{0,1},{1,2},{2,3},{3,4},{4,5},{5,6},{6,7},{7,8},{8,9},{9,10},{10,1... | collective-permute-start | bytes 589832 | tf_op jit(solution)/shard_map/ppermute | solution.py:490
  27.3 2.7 %collective-permute-done.3.refs_3_ = f32[3,64,256]{2,1,0:T(8,128)S(1)} collective-permute-done((f32[3,64,256]{2,1,0:T(8,128)S(1)}, f32[3,64,256]{2,1,0:T(8,128)S(1)}, u32[]{:S(2)}, u32[]{:S(2)}) %collective-permute-start.3) | collective-permute-done | bytes 196640 | tf_op jit(solution)/shard_map/ppermute | solution.py:490
  30.0 0.0 copy-start.4
  30.0 5.9 %collective-permute-done.2.refs_1_ = f32[3,64,256]{2,1,0:T(8,128)S(1)} collective-permute-done((f32[3,64,256]{2,1,0:T(8,128)S(1)}, f32[3,64,256]{2,1,0:T(8,128)S(1)}, u32[]{:S(2)}, u32[]{:S(2)}) %collective-permute-start.2) | collective-permute-done | bytes 196640 | tf_op jit(solution)/shard_map/ppermute | solution.py:490
  35.9 0.0 copy-start.5
  35.9 0.0 copy-done.3
  35.9 0.0 copy-done.4
  35.9 0.7 copy-done.5
  36.6 31.1 %shard_map.178 = (f32[1280,256]{1,0:T(8,128)}, f32[1280,256]{1,0:T(8,128)}, f32[3,64,256]{2,1,0:T(8,128)}, f32[3,64,256]{2,1,0:T(8,128)}, f32[3,64,256]{2,1,0:T(8,128)}) custom-call(s32[1]{0:T(128)} %bitcast.refs_0_.core, f32[3,64,256]{2,1,0:T(8,128)} %copy-done.5, f32[3,64,256]{2,1,0:T(8,128)} %copy-done.3, f32[3,64,256]{2,1,0:T(8,128)} %copy-done.4, ...), custom_call_target="tpu_custom_call" | custom-call | tf_op jit(solution)/shard_map/pallas_call | solution.py:469
  67.7 1.9 %collective-permute-start.4 = (f32[1280,256]{1,0:T(8,128)}, f32[1280,256]{1,0:T(8,128)S(1)}, u32[]{:S(2)}, u32[]{:S(2)}) collective-permute-start(f32[1280,256]{1,0:T(8,128)} %get-tuple-element.30), channel_id=1, source_target_pairs={{0,1},{1,0},{2,3},{3,2},{4,5},{5,4},{6,7},{7,6},{8,9},{9,8},{10,11... | collective-permute-start | bytes 3932168 | tf_op jit(solution)/shard_map/ppermute | solution.py:508
  69.6 3.2 %collective-permute-done.4 = f32[1280,256]{1,0:T(8,128)S(1)} collective-permute-done((f32[1280,256]{1,0:T(8,128)}, f32[1280,256]{1,0:T(8,128)S(1)}, u32[]{:S(2)}, u32[]{:S(2)}) %collective-permute-start.4) | collective-permute-done | bytes 1310752 | tf_op jit(solution)/shard_map/ppermute | solution.py:508
  72.8 1.5 add.9
  74.3 26.1 %all_to_all.20 = f32[16,80,256]{2,1,0:T(8,128)S(1)} all-to-all(f32[16,80,256]{2,1,0:T(8,128)S(1)} %bitcast.19), channel_id=1, replica_groups=mesh['z'=16,'xl'=2,'y'=4,'xh'=2,'co'=2] {'xl','y','xh'}, dimensions={0} | all-to-all | bytes 2621440 | tf_op jit(solution)/shard_map/all_to_all | solution.py:497
  100.4 0.1 reduce_sum.18
  100.6 19.5 %all_to_all.21 = f32[16,5,256]{2,1,0:T(8,128)S(1)} all-to-all(f32[16,5,256]{2,1,0:T(8,128)S(1)} %reshape.45), channel_id=1, replica_groups=mesh['z'=16,'xl'=2,'y'=4,'xh'=2,'co'=2] {'z'}, dimensions={0} | all-to-all | bytes 163840 | tf_op jit(solution)/shard_map/all_to_all | solution.py:497
  120.1 17.1 %all_to_all.22 = f32[16,5,256]{2,1,0:T(8,128)S(1)} all-to-all(f32[16,5,256]{2,1,0:T(8,128)S(1)} %broadcast_in_dim.6), channel_id=1, replica_groups=mesh['z'=16,'xl'=2,'y'=4,'xh'=2,'co'=2] {'z'}, dimensions={0} | all-to-all | bytes 163840 | tf_op jit(solution)/shard_map/all_to_all | solution.py:497
  137.3 0.1 broadcast_in_dim.7
  137.4 0.0 copy-start.10
  137.4 0.0 copy-start.9
  137.4 0.0 copy-start.6
  137.4 20.3 %all_to_all.23 = f32[16,80,256]{2,1,0:T(8,128)S(1)} all-to-all(f32[16,80,256]{2,1,0:T(8,128)S(1)} %broadcast_in_dim.7), channel_id=1, replica_groups=mesh['z'=16,'xl'=2,'y'=4,'xh'=2,'co'=2] {'xl','y','xh'}, dimensions={0} | all-to-all | bytes 2621440 | tf_op jit(solution)/shard_map/all_to_all | solution.py:497
  157.7 0.0 copy-start
  157.7 1.9 %collective-permute-start.5 = (f32[1280,256]{1,0:T(8,128)S(1)}, f32[1280,256]{1,0:T(8,128)S(1)}, u32[]{:S(2)}, u32[]{:S(2)}) collective-permute-start(f32[1280,256]{1,0:T(8,128)S(1)} %bitcast.17), channel_id=1, source_target_pairs={{0,1},{1,0},{2,3},{3,2},{4,5},{5,4},{6,7},{7,6},{8,9},{9,8},{10,11... | collective-permute-start | bytes 3932168 | tf_op jit(solution)/shard_map/ppermute | solution.py:516
  159.7 0.0 copy-done.10
  159.7 4.3 %collective-permute-start.6 = (f32[3,64,256]{2,1,0:T(8,128)S(1)}, f32[3,64,256]{2,1,0:T(8,128)S(1)}, u32[]{:S(2)}, u32[]{:S(2)}) collective-permute-start(f32[3,64,256]{2,1,0:T(8,128)S(1)} %copy-done.10), channel_id=1, source_target_pairs={{0,15},{1,0},{2,1},{3,2},{4,3},{5,4},{6,5},{7,6},{8,7},{9,8},{10,9... | collective-permute-start | bytes 589832 | tf_op jit(solution)/shard_map/ppermute | solution.py:490
  163.9 0.0 copy-done.9
  163.9 1.9 %collective-permute-start.7 = (f32[3,64,256]{2,1,0:T(8,128)S(1)}, f32[3,64,256]{2,1,0:T(8,128)S(1)}, u32[]{:S(2)}, u32[]{:S(2)}) collective-permute-start(f32[3,64,256]{2,1,0:T(8,128)S(1)} %copy-done.9), channel_id=1, source_target_pairs={{0,1},{1,2},{2,3},{3,4},{4,5},{5,6},{6,7},{7,8},{8,9},{9,10},{10,1... | collective-permute-start | bytes 589832 | tf_op jit(solution)/shard_map/ppermute | solution.py:490
  165.9 1.2 collective-permute-done.6
  167.1 7.4 %collective-permute-done.7 = f32[3,64,256]{2,1,0:T(8,128)S(1)} collective-permute-done((f32[3,64,256]{2,1,0:T(8,128)S(1)}, f32[3,64,256]{2,1,0:T(8,128)S(1)}, u32[]{:S(2)}, u32[]{:S(2)}) %collective-permute-start.7) | collective-permute-done | bytes 196640 | tf_op jit(solution)/shard_map/ppermute | solution.py:490
  174.5 0.0 copy-done.6
  174.6 0.0 copy-start.1
  174.6 3.4 %collective-permute-start.9 = (f32[64,256]{1,0:T(8,128)S(1)}, f32[64,256]{1,0:T(8,128)S(1)}, u32[]{:S(2)}, u32[]{:S(2)}) collective-permute-start(f32[64,256]{1,0:T(8,128)S(1)} %get-tuple-element.44), channel_id=1, source_target_pairs={{0,16},{16,32},{32,48},{48,64},{64,80},{80,96},{96,112},{112,128},... | collective-permute-start | bytes 196616 | tf_op jit(solution)/shard_map/ppermute | solution.py:490
  178.1 2.4 %collective-permute-start.8 = (f32[64,256]{1,0:T(8,128)S(1)}, f32[64,256]{1,0:T(8,128)S(1)}, u32[]{:S(2)}, u32[]{:S(2)}) collective-permute-start(f32[64,256]{1,0:T(8,128)S(1)} %get-tuple-element.45), channel_id=1, source_target_pairs={{0,496},{16,0},{32,16},{48,32},{64,48},{80,64},{96,80},{112,96},{1... | collective-permute-start | bytes 196616 | tf_op jit(solution)/shard_map/ppermute | solution.py:490
  180.5 0.3 collective-permute-done.9.after
  180.8 0.0 copy-start.7
  180.8 4.3 %collective-permute-done.8.before = f32[64,256]{1,0:T(8,128)S(1)} collective-permute-done((f32[64,256]{1,0:T(8,128)S(1)}, f32[64,256]{1,0:T(8,128)S(1)}, u32[]{:S(2)}, u32[]{:S(2)}) %collective-permute-start.8) | collective-permute-done | bytes 65568 | tf_op jit(solution)/shard_map/ppermute | solution.py:490
  185.1 0.0 copy-start.8
  185.1 0.0 collective-permute-done.5.other
  185.1 0.0 copy-done
  185.1 0.0 copy-done.1
  185.1 0.0 copy-done.7
  185.2 0.6 copy-done.8
  185.7 0.0 copy-start.2
  185.7 1.1 copy-done.2
  186.8 3.3 %shard_map.179 = (f32[1,1]{1,0:T(1,128)}, f32[8,8,192]{2,1,0:T(8,128)}, f32[192,256]{1,0:T(8,128)}, f32[1,256]{1,0:T(1,128)}, f32[256,768]{1,0:T(8,128)}, /*inde...) custom-call(s32[1]{0:T(128)} %bitcast.refs_0_.core, ...), custom_call_target="tpu_custom_call" | custom-call | tf_op jit(solution)/shard_map/pallas_call | solution.py:481
  (6 shorter events, 0.1 us)
Async XLA Ops:
  2.5 10.0 %collective-permute-start.1 = (f32[64,256]{1,0:T(8,128)}, f32[64,256]{1,0:T(8,128)S(1)}, u32[]{:S(2)}, u32[]{:S(2)}) collective-permute-start(f32[64,256]{1,0:T(8,128)} %get-tuple-element.27), channel_id=1, source_target_pairs={{0,496},{16,0},{32,16},{48,32},{64,48},{80,64},{96,80},{112,96},{1... | collective-permute-start | bytes 196616 | tf_op jit(solution)/shard_map/ppermute | solution.py:490
  10.3 9.4 %collective-permute-start = (f32[64,256]{1,0:T(8,128)}, f32[64,256]{1,0:T(8,128)S(1)}, u32[]{:S(2)}, u32[]{:S(2)}) collective-permute-start(f32[64,256]{1,0:T(8,128)} %get-tuple-element.27), channel_id=1, source_target_pairs={{0,16},{16,32},{32,48},{48,64},{64,80},{80,96},{96,112},{112,128},... | collective-permute-start | bytes 196616 | tf_op jit(solution)/shard_map/ppermute | solution.py:490
  20.5 15.4 %copy-start.3 = (f32[3,64,256]{2,1,0:T(8,128)}, f32[3,64,256]{2,1,0:T(8,128)S(1)}, u32[]{:S(2)}) copy-start(f32[3,64,256]{2,1,0:T(8,128)S(1)} %pad_maximum_fusion.refs_2_) | copy-start | bytes 589828
  20.6 9.4 %collective-permute-start.3 = (f32[3,64,256]{2,1,0:T(8,128)S(1)}, f32[3,64,256]{2,1,0:T(8,128)S(1)}, u32[]{:S(2)}, u32[]{:S(2)}) collective-permute-start(f32[3,64,256]{2,1,0:T(8,128)S(1)} %pad_maximum_fusion.refs_2_), channel_id=1, source_target_pairs={{0,15},{1,0},{2,1},{3,2},{4,3},{5,4},{6,5},{7,6},{8,7},{9,8},{10,9... | collective-permute-start | bytes 589832 | tf_op jit(solution)/shard_map/ppermute | solution.py:490
  25.3 10.6 %collective-permute-start.2 = (f32[3,64,256]{2,1,0:T(8,128)S(1)}, f32[3,64,256]{2,1,0:T(8,128)S(1)}, u32[]{:S(2)}, u32[]{:S(2)}) collective-permute-start(f32[3,64,256]{2,1,0:T(8,128)S(1)} %pad_maximum_fusion.refs_2_), channel_id=1, source_target_pairs={{0,1},{1,2},{2,3},{3,4},{4,5},{5,6},{6,7},{7,8},{8,9},{9,10},{10,1... | collective-permute-start | bytes 589832 | tf_op jit(solution)/shard_map/ppermute | solution.py:490
  30.0 6.0 %copy-start.4 = (f32[3,64,256]{2,1,0:T(8,128)}, f32[3,64,256]{2,1,0:T(8,128)S(1)}, u32[]{:S(2)}) copy-start(f32[3,64,256]{2,1,0:T(8,128)S(1)} %collective-permute-done.3.refs_3_) | copy-start | bytes 589828
  35.9 0.7 copy-start.5
  67.7 5.1 %collective-permute-start.4 = (f32[1280,256]{1,0:T(8,128)}, f32[1280,256]{1,0:T(8,128)S(1)}, u32[]{:S(2)}, u32[]{:S(2)}) collective-permute-start(f32[1280,256]{1,0:T(8,128)} %get-tuple-element.30), channel_id=1, source_target_pairs={{0,1},{1,0},{2,3},{3,2},{4,5},{5,4},{6,7},{7,6},{8,9},{9,8},{10,11... | collective-permute-start | bytes 3932168 | tf_op jit(solution)/shard_map/ppermute | solution.py:508
  137.4 22.3 %copy-start.10 = (f32[3,64,256]{2,1,0:T(8,128)S(1)}, f32[3,64,256]{2,1,0:T(8,128)}, u32[]{:S(2)}) copy-start(f32[3,64,256]{2,1,0:T(8,128)} %get-tuple-element.32) | copy-start | bytes 589828
  137.4 26.5 %copy-start.9 = (f32[3,64,256]{2,1,0:T(8,128)S(1)}, f32[3,64,256]{2,1,0:T(8,128)}, u32[]{:S(2)}) copy-start(f32[3,64,256]{2,1,0:T(8,128)} %get-tuple-element.33) | copy-start | bytes 589828
  137.4 37.1 %copy-start.6 = (f32[3,64,256]{2,1,0:T(8,128)S(1)}, f32[3,64,256]{2,1,0:T(8,128)}, u32[]{:S(2)}) copy-start(f32[3,64,256]{2,1,0:T(8,128)} %get-tuple-element.31) | copy-start | bytes 589828
  157.7 27.4 %copy-start = (f32[16,80,256]{2,1,0:T(8,128)}, f32[16,80,256]{2,1,0:T(8,128)S(1)}, u32[]{:S(2)}) copy-start(f32[16,80,256]{2,1,0:T(8,128)S(1)} %all_to_all.23) | copy-start | bytes 3932164
  157.7 27.4 %collective-permute-start.5 = (f32[1280,256]{1,0:T(8,128)S(1)}, f32[1280,256]{1,0:T(8,128)S(1)}, u32[]{:S(2)}, u32[]{:S(2)}) collective-permute-start(f32[1280,256]{1,0:T(8,128)S(1)} %bitcast.17), channel_id=1, source_target_pairs={{0,1},{1,0},{2,3},{3,2},{4,5},{5,4},{6,7},{7,6},{8,9},{9,8},{10,11... | collective-permute-start | bytes 3932168 | tf_op jit(solution)/shard_map/ppermute | solution.py:516
  159.7 7.4 %collective-permute-start.6 = (f32[3,64,256]{2,1,0:T(8,128)S(1)}, f32[3,64,256]{2,1,0:T(8,128)S(1)}, u32[]{:S(2)}, u32[]{:S(2)}) collective-permute-start(f32[3,64,256]{2,1,0:T(8,128)S(1)} %copy-done.10), channel_id=1, source_target_pairs={{0,15},{1,0},{2,1},{3,2},{4,3},{5,4},{6,5},{7,6},{8,7},{9,8},{10,9... | collective-permute-start | bytes 589832 | tf_op jit(solution)/shard_map/ppermute | solution.py:490
  163.9 10.6 %collective-permute-start.7 = (f32[3,64,256]{2,1,0:T(8,128)S(1)}, f32[3,64,256]{2,1,0:T(8,128)S(1)}, u32[]{:S(2)}, u32[]{:S(2)}) collective-permute-start(f32[3,64,256]{2,1,0:T(8,128)S(1)} %copy-done.9), channel_id=1, source_target_pairs={{0,1},{1,2},{2,3},{3,4},{4,5},{5,6},{6,7},{7,8},{8,9},{9,10},{10,1... | collective-permute-start | bytes 589832 | tf_op jit(solution)/shard_map/ppermute | solution.py:490
  174.6 10.5 %copy-start.1 = (f32[3,64,256]{2,1,0:T(8,128)}, f32[3,64,256]{2,1,0:T(8,128)S(1)}, u32[]{:S(2)}) copy-start(f32[3,64,256]{2,1,0:T(8,128)S(1)} %add_add_fusion.wide) | copy-start | bytes 589828
  174.6 6.2 %collective-permute-start.9 = (f32[64,256]{1,0:T(8,128)S(1)}, f32[64,256]{1,0:T(8,128)S(1)}, u32[]{:S(2)}, u32[]{:S(2)}) collective-permute-start(f32[64,256]{1,0:T(8,128)S(1)} %get-tuple-element.44), channel_id=1, source_target_pairs={{0,16},{16,32},{32,48},{48,64},{64,80},{80,96},{96,112},{112,128},... | collective-permute-start | bytes 196616 | tf_op jit(solution)/shard_map/ppermute | solution.py:490
  178.1 7.1 %collective-permute-start.8 = (f32[64,256]{1,0:T(8,128)S(1)}, f32[64,256]{1,0:T(8,128)S(1)}, u32[]{:S(2)}, u32[]{:S(2)}) collective-permute-start(f32[64,256]{1,0:T(8,128)S(1)} %get-tuple-element.45), channel_id=1, source_target_pairs={{0,496},{16,0},{32,16},{48,32},{64,48},{80,64},{96,80},{112,96},{1... | collective-permute-start | bytes 196616 | tf_op jit(solution)/shard_map/ppermute | solution.py:490
  180.8 4.4 %copy-start.7 = (f32[64,256]{1,0:T(8,128)}, f32[64,256]{1,0:T(8,128)S(1)}, u32[]{:S(2)}) copy-start(f32[64,256]{1,0:T(8,128)S(1)} %collective-permute-done.9.after) | copy-start | bytes 196612
  185.1 0.6 copy-start.8
  185.7 1.1 copy-start.2

commit v3 on v2

--- a/solution.py
+++ b/solution.py
@@ -12,7 +12,7 @@
 INTERPRET = False
 
 EMBED, ATTEND, OUTPUT, EXPAND, REDUCE, DECODE, SMALL, ROWS = 0, 192, 960, 1216, 1728, 2240, 2432, 2560
-VMEM_LIMIT = 60 * 1024 * 1024
+MIB = 1024 * 1024
 
 
 def split(x):
@@ -355,25 +355,28 @@
     stencil_back(ext_ref, back_ref, g, m, n)
 
 
+NAMES = ("embed", "attend", "output", "expand", "reduce", "decode")
+WIDTHS = {"embed": (256, 256), "attend": (256, 768), "output": (256, 256), "expand": (256, 512), "reduce": (512, 256), "decode": (256, 256)}
+
+
+def weights_kernel(*refs):
+    inputs, w, strip = dict(zip(NAMES, refs[:6])), dict(zip(NAMES, refs[6:12])), refs[12]
+    for name in NAMES:
+        if name in ("embed", "decode"):
+            put(w[name], 0, reorder(strip, inputs[name][...]))
+            put(w[name], 192, jnp.zeros((64, 256), F32))
+        else:
+            put(w[name], 0, inputs[name][...])
+
+
 def main_kernel(*refs):
-    (core, low, own, high, goal, embed, gain1, attend, output, gain2, expand, reduce, decode) = refs[:13]
+    (core, low, own, high, goal, gain1, gain2) = refs[:7]
+    w = dict(zip(NAMES, refs[7:13]))
     (kept, sent, out_low, out_own, out_high) = refs[13:18]
     scratch = list(refs[18:])
     grads = scratch.pop(0)
-    w = {}
-    for name in ("embed", "attend", "output", "expand", "reduce", "decode"):
-        w[name] = scratch.pop(0)
-    strip = scratch.pop(0)
     ext0, back0, ext1, back1, dkv0, dkv1, dq0, dq1 = scratch[:8]
     r0, r1 = scratch[8:17], scratch[17:26]
-    put(w["embed"], 0, reorder(strip, embed[...]))
-    put(w["decode"], 0, reorder(strip, decode[...]))
-    put(w["embed"], 192, jnp.zeros((64, 256), F32))
-    put(w["decode"], 192, jnp.zeros((64, 256), F32))
-    put(w["attend"], 0, attend[...])
-    put(w["output"], 0, output[...])
-    put(w["expand"], 0, expand[...])
-    put(w["reduce"], 0, reduce[...])
     g1, g2 = gain1[...], gain2[...]
     spots = [
         (by, bx, (px * 2 + py) * 16, ((2 * bx + px) * 6 + 2 * by + py) * 16)
@@ -429,12 +432,12 @@
     return jax.ShapeDtypeStruct(shape, dtype)
 
 
-def call(kernel, outs, scratch, **more):
+def call(kernel, outs, scratch, limit, **more):
     return pl.pallas_call(
         kernel,
         out_shape=outs,
         scratch_shapes=scratch,
-        compiler_params=pltpu.CompilerParams(vmem_limit_bytes=VMEM_LIMIT),
+        compiler_params=pltpu.CompilerParams(vmem_limit_bytes=limit * MIB),
         interpret=INTERPRET,
         **more,
     )
@@ -442,10 +445,17 @@
 
 def prepare(field, target):
     scratch = [pltpu.VMEM((64, 192), F32), pltpu.VMEM((192, 128), F32)]
-    return call(prepare_kernel, (arr(64, 256), arr(64, 256)), scratch)(field, target)
-
-
-def work(core, low, own, high, goal, weights):
+    return call(prepare_kernel, (arr(64, 256), arr(64, 256)), scratch, 4)(field, target)
+
+
+def split_weights(weights):
+    embed, _, attend, output, _, expand, reduce, decode = weights
+    outs = [arr(2, *WIDTHS[name], dtype=BF16) for name in NAMES]
+    inputs = (embed, attend, output, expand, reduce, decode.T)
+    return call(weights_kernel, outs, [pltpu.VMEM((2, 192, 128), F32)], 14)(*inputs)
+
+
+def work(core, low, own, high, goal, gains, halves):
     def V(*shape, dtype=F32):
         return pltpu.VMEM(shape, dtype)
 
@@ -456,17 +466,14 @@
         ]
 
     scratch = [
-        V(ROWS, 256), V(2, 256, 256, dtype=BF16), V(2, 256, 768, dtype=BF16), V(2, 256, 256, dtype=BF16),
-        V(2, 256, 512, dtype=BF16), V(2, 512, 256, dtype=BF16), V(2, 256, 256, dtype=BF16),
-        V(2, 192, 128),
+        V(ROWS, 256),
         V(576, 256), V(576, 256), V(256, 256), V(256, 256), V(576, 512), V(256, 512), V(256, 256), V(64, 256),
         *kept(576, 256, 4), *kept(256, 64, 2),
     ]
     half = arr(ROWS // 2, 256)
     outs = (half, half, arr(3, 64, 256), arr(3, 64, 256), arr(3, 64, 256))
-    embed, gain1, attend, output, gain2, expand, reduce, decode = weights
-    args = (embed, gain1.reshape(1, 256), attend, output, gain2.reshape(1, 256), expand, reduce, decode.T)
-    return call(main_kernel, outs, scratch, in_specs=places(1, 12))(core, low, own, high, goal, *args)
+    args = (gains[0].reshape(1, 256), gains[1].reshape(1, 256), *halves)
+    return call(main_kernel, outs, scratch, 24, in_specs=places(1, 12))(core, low, own, high, goal, *args)
 
 
 def finish(core, mine, other, wide, before, after):
@@ -478,7 +485,7 @@
         pltpu.VMEM((2, 192, 128), F32), pltpu.VMEM((ROWS, 256), F32),
         pltpu.VMEM((192, 128), F32), pltpu.VMEM((128, 192), F32),
     ]
-    return call(finish_kernel, outs, scratch, in_specs=places(1, 5))(core, mine, other, wide, before, after)
+    return call(finish_kernel, outs, scratch, 16, in_specs=places(1, 5))(core, mine, other, wide, before, after)
 
 
 AXES = ("z", "xl", "y", "xh", "co")
@@ -501,10 +508,11 @@
     core = lax.axis_index("co").reshape(1)
     half = ROWS // 2
     swapped = [(0, 1), (1, 0)]
+    halves = split_weights(weights)
     tokens, goal = prepare(field, target)
     own = jnp.stack([shift(tokens, GX, 1), tokens, shift(tokens, GX, -1)])
     low, high = shift(own, GY, 1), shift(own, GY, -1)
-    kept, sent, back_low, back_own, back_high = work(core, low, own, high, goal, weights)
+    kept, sent, back_low, back_own, back_high = work(core, low, own, high, goal, (weights[1], weights[4]), halves)
     total = kept + lax.ppermute(sent, "co", swapped)
     back_low, back_high = shift(back_low, GY, -1), shift(back_high, GY, 1)
     wide = back_own + (back_low + back_high)

time: 191 us -> 183 us (0.958)
  waiting for transfers between devices: 32.7 us -> 25.6 us
  Pallas kernels: 36.2 us -> 30.1 us
  local copies, waits for them, and re-layouts: 2.54 us -> 7.87 us
  other arithmetic: 2.48 us -> 0.33 us
    ppermute x8, waiting for transfers between devices: 29.5 us -> 22.6 us  [shift(): lax.ppermute(x, axes, [(i, (i + step) % count) for i in range(count)])]
    pallas_call x3 -> x4, Pallas kernels: 36.2 us -> 30.1 us  [the longest x1 27.2 us: work(): call(main_kernel, outs, scratch, 24, in_specs=places(1, 12))]
    unnamed x22 -> x20, local copies, waits for them, and re-layouts: 2.37 us -> 7.7 us
  transfers between devices with their start and end apart: 10 -> 10, of which waited for: 9 -> 7; matrix products, arithmetic and copies ran while one was open for 0% -> 0% of each run, Pallas kernels for 0% -> 0%
where the time goes in v3:
time: 183 us; the launch traced here: 182 us
  blocking collectives  84.8 us (46%)
  starting transfers between devices  32.2 us (18%)
  Pallas kernels  30.1 us (16%)
  waiting for transfers between devices  25.6 us (14%)
  local copies, waits for them, and re-layouts  7.87 us (4%)
    all_to_all x4, blocking collectives, swap(): return lax.all_to_all(x, axes, 0, 0, tiled=True)  84.8 us
    ppermute x8, starting transfers between devices, shift(): lax.ppermute(x, axes, [(i, (i + step) % count) for i in range(count)])  28.4 us
    pallas_call x1, Pallas kernels, work(): call(main_kernel, outs, scratch, 24, in_specs=places(1, 12))  27.2 us
    ppermute x8, waiting for transfers between devices, shift(): lax.ppermute(x, axes, [(i, (i + step) % count) for i in range(count)])  22.6 us
    unnamed x20, local copies, waits for them, and re-layouts  7.7 us
  transfers between devices with their start and end apart: 10, of which 7 were waited for; matrix products, arithmetic and copies ran while one was open for 0% of the time, Pallas kernels for 0%

profile of v3, /device:TPU:2, one launch (start us, length us, event | category | flops | bytes accessed | tf_op | source)
XLA Modules:
  0.0 181.8 jit_solution(16074896063584389733)
XLA Ops:
  0.6 0.0 copy-start.6
  0.7 0.8 copy-done.6
  1.5 0.0 copy-start.7
  1.5 0.8 copy-done.7
  2.3 0.3 shard_map.177
  2.7 7.8 %collective-permute-start.1 = (f32[64,256]{1,0:T(8,128)S(1)}, f32[64,256]{1,0:T(8,128)S(1)}, u32[]{:S(2)}, u32[]{:S(2)}) collective-permute-start(f32[64,256]{1,0:T(8,128)S(1)} %get-tuple-element.33), channel_id=1, source_target_pairs={{0,496},{16,0},{32,16},{48,32},{64,48},{80,64},{96,80},{112,96},{1... | collective-permute-start | bytes 196616 | tf_op jit(solution)/shard_map/ppermute | solution.py:497
  10.5 1.9 %collective-permute-start = (f32[64,256]{1,0:T(8,128)S(1)}, f32[64,256]{1,0:T(8,128)S(1)}, u32[]{:S(2)}, u32[]{:S(2)}) collective-permute-start(f32[64,256]{1,0:T(8,128)S(1)} %get-tuple-element.33), channel_id=1, source_target_pairs={{0,16},{16,32},{32,48},{48,64},{64,80},{80,96},{96,112},{112,128},... | collective-permute-start | bytes 196616 | tf_op jit(solution)/shard_map/ppermute | solution.py:497
  12.4 0.0 collective-permute-done.1
  12.4 7.3 %collective-permute-done = f32[64,256]{1,0:T(8,128)S(1)} collective-permute-done((f32[64,256]{1,0:T(8,128)S(1)}, f32[64,256]{1,0:T(8,128)S(1)}, u32[]{:S(2)}, u32[]{:S(2)}) %collective-permute-start) | collective-permute-done | bytes 65568 | tf_op jit(solution)/shard_map/ppermute | solution.py:497
  19.7 0.0 copy-start.8
  19.7 0.0 copy-start.9
  19.7 4.8 %collective-permute-start.3 = (f32[3,64,256]{2,1,0:T(8,128)S(1)}, f32[3,64,256]{2,1,0:T(8,128)S(1)}, u32[]{:S(2)}, u32[]{:S(2)}) collective-permute-start(f32[3,64,256]{2,1,0:T(8,128)S(1)} %pad_maximum_fusion.refs_2_), channel_id=1, source_target_pairs={{0,15},{1,0},{2,1},{3,2},{4,3},{5,4},{6,5},{7,6},{8,7},{9,8},{10,9... | collective-permute-start | bytes 589832 | tf_op jit(solution)/shard_map/ppermute | solution.py:497
  24.5 1.9 %collective-permute-start.2 = (f32[3,64,256]{2,1,0:T(8,128)S(1)}, f32[3,64,256]{2,1,0:T(8,128)S(1)}, u32[]{:S(2)}, u32[]{:S(2)}) collective-permute-start(f32[3,64,256]{2,1,0:T(8,128)S(1)} %pad_maximum_fusion.refs_2_), channel_id=1, source_target_pairs={{0,1},{1,2},{2,3},{3,4},{4,5},{5,6},{6,7},{7,8},{8,9},{9,10},{10,1... | collective-permute-start | bytes 589832 | tf_op jit(solution)/shard_map/ppermute | solution.py:497
  26.4 0.0 copy-start
  26.5 1.1 copy-done
  27.6 0.0 copy-start.1
  27.6 1.0 copy-done.1
  28.6 0.0 copy-start.2
  28.6 1.0 copy-done.2
  29.7 0.0 copy-start.3
  29.7 0.9 copy-done.3
  30.6 0.0 copy-start.4
  30.6 0.9 copy-done.4
  31.5 0.0 copy-start.5
  31.5 0.9 copy-done.5
  32.5 0.6 shard_map.178
  33.1 0.0 collective-permute-done.3.refs_3_
  33.1 2.0 %collective-permute-done.2.refs_1_ = f32[3,64,256]{2,1,0:T(8,128)S(1)} collective-permute-done((f32[3,64,256]{2,1,0:T(8,128)S(1)}, f32[3,64,256]{2,1,0:T(8,128)S(1)}, u32[]{:S(2)}, u32[]{:S(2)}) %collective-permute-start.2) | collective-permute-done | bytes 196640 | tf_op jit(solution)/shard_map/ppermute | solution.py:497
  35.1 0.0 copy-done.8
  35.1 0.0 copy-done.9
  35.1 27.2 %shard_map.179 = (f32[1280,256]{1,0:T(8,128)S(1)}, f32[1280,256]{1,0:T(8,128)S(1)}, f32[3,64,256]{2,1,0:T(8,128)S(1)}, f32[3,64,256]{2,1,0:T(8,128)S(1)}, f32[3,64,256]{2,1,0:T(8,128)S(1)}) custom-call(s32[1]{0:T(128)} %bitcast.refs_0_.core, f32[3,64,256]{2,1,0:T(8,128)S(1)} %collective-permute-done.2.refs_1_, f32[3,64,256]{2,1,0:T(8,128)S(1)} %pad_maximum_fusion.refs_2_, ...), custom_call_target="tpu_custom_call" | custom-call | tf_op jit(solution)/shard_map/pallas_call | solution.py:476
  62.3 1.9 %collective-permute-start.4 = (f32[1280,256]{1,0:T(8,128)S(1)}, f32[1280,256]{1,0:T(8,128)S(1)}, u32[]{:S(2)}, u32[]{:S(2)}) collective-permute-start(f32[1280,256]{1,0:T(8,128)S(1)} %get-tuple-element.42), channel_id=1, source_target_pairs={{0,1},{1,0},{2,3},{3,2},{4,5},{5,4},{6,7},{7,6},{8,9},{9,8},{10,11... | collective-permute-start | bytes 3932168 | tf_op jit(solution)/shard_map/ppermute | solution.py:516
  64.2 3.0 %collective-permute-done.4 = f32[1280,256]{1,0:T(8,128)S(1)} collective-permute-done((f32[1280,256]{1,0:T(8,128)S(1)}, f32[1280,256]{1,0:T(8,128)S(1)}, u32[]{:S(2)}, u32[]{:S(2)}) %collective-permute-start.4) | collective-permute-done | bytes 1310752 | tf_op jit(solution)/shard_map/ppermute | solution.py:516
  67.2 0.2 add.9
  67.4 28.1 %all_to_all.20 = f32[16,80,256]{2,1,0:T(8,128)S(1)} all-to-all(f32[16,80,256]{2,1,0:T(8,128)S(1)} %bitcast.23), channel_id=1, replica_groups=mesh['z'=16,'xl'=2,'y'=4,'xh'=2,'co'=2] {'xl','y','xh'}, dimensions={0} | all-to-all | bytes 2621440 | tf_op jit(solution)/shard_map/all_to_all | solution.py:504
  95.5 0.1 reduce_sum.18
  95.6 19.5 %all_to_all.21 = f32[16,5,256]{2,1,0:T(8,128)S(1)} all-to-all(f32[16,5,256]{2,1,0:T(8,128)S(1)} %reshape.45), channel_id=1, replica_groups=mesh['z'=16,'xl'=2,'y'=4,'xh'=2,'co'=2] {'z'}, dimensions={0} | all-to-all | bytes 163840 | tf_op jit(solution)/shard_map/all_to_all | solution.py:504
  115.1 16.5 %all_to_all.22 = f32[16,5,256]{2,1,0:T(8,128)S(1)} all-to-all(f32[16,5,256]{2,1,0:T(8,128)S(1)} %broadcast_in_dim.6), channel_id=1, replica_groups=mesh['z'=16,'xl'=2,'y'=4,'xh'=2,'co'=2] {'z'}, dimensions={0} | all-to-all | bytes 163840 | tf_op jit(solution)/shard_map/all_to_all | solution.py:504
  131.7 0.1 broadcast_in_dim.7
  131.8 20.7 %all_to_all.23 = f32[16,80,256]{2,1,0:T(8,128)S(1)} all-to-all(f32[16,80,256]{2,1,0:T(8,128)S(1)} %broadcast_in_dim.7), channel_id=1, replica_groups=mesh['z'=16,'xl'=2,'y'=4,'xh'=2,'co'=2] {'xl','y','xh'}, dimensions={0} | all-to-all | bytes 2621440 | tf_op jit(solution)/shard_map/all_to_all | solution.py:504
  152.5 1.9 %collective-permute-start.5 = (f32[1280,256]{1,0:T(8,128)S(1)}, f32[1280,256]{1,0:T(8,128)S(1)}, u32[]{:S(2)}, u32[]{:S(2)}) collective-permute-start(f32[1280,256]{1,0:T(8,128)S(1)} %bitcast.17), channel_id=1, source_target_pairs={{0,1},{1,0},{2,3},{3,2},{4,5},{5,4},{6,7},{7,6},{8,9},{9,8},{10,11... | collective-permute-start | bytes 3932168 | tf_op jit(solution)/shard_map/ppermute | solution.py:524
  154.4 4.3 %collective-permute-start.6 = (f32[3,64,256]{2,1,0:T(8,128)S(1)}, f32[3,64,256]{2,1,0:T(8,128)S(1)}, u32[]{:S(2)}, u32[]{:S(2)}) collective-permute-start(f32[3,64,256]{2,1,0:T(8,128)S(1)} %get-tuple-element.44), channel_id=1, source_target_pairs={{0,15},{1,0},{2,1},{3,2},{4,3},{5,4},{6,5},{7,6},{8,7},{9,8},{10,9... | collective-permute-start | bytes 589832 | tf_op jit(solution)/shard_map/ppermute | solution.py:497
  158.7 1.9 %collective-permute-start.7 = (f32[3,64,256]{2,1,0:T(8,128)S(1)}, f32[3,64,256]{2,1,0:T(8,128)S(1)}, u32[]{:S(2)}, u32[]{:S(2)}) collective-permute-start(f32[3,64,256]{2,1,0:T(8,128)S(1)} %get-tuple-element.45), channel_id=1, source_target_pairs={{0,1},{1,2},{2,3},{3,4},{4,5},{5,6},{6,7},{7,8},{8,9},{9,10},{10,1... | collective-permute-start | bytes 589832 | tf_op jit(solution)/shard_map/ppermute | solution.py:497
  160.6 1.2 collective-permute-done.6
  161.8 7.4 %collective-permute-done.7 = f32[3,64,256]{2,1,0:T(8,128)S(1)} collective-permute-done((f32[3,64,256]{2,1,0:T(8,128)S(1)}, f32[3,64,256]{2,1,0:T(8,128)S(1)}, u32[]{:S(2)}, u32[]{:S(2)}) %collective-permute-start.7) | collective-permute-done | bytes 196640 | tf_op jit(solution)/shard_map/ppermute | solution.py:497
  169.3 3.4 %collective-permute-start.9 = (f32[64,256]{1,0:T(8,128)S(1)}, f32[64,256]{1,0:T(8,128)S(1)}, u32[]{:S(2)}, u32[]{:S(2)}) collective-permute-start(f32[64,256]{1,0:T(8,128)S(1)} %get-tuple-element.56), channel_id=1, source_target_pairs={{0,16},{16,32},{32,48},{48,64},{64,80},{80,96},{96,112},{112,128},... | collective-permute-start | bytes 196616 | tf_op jit(solution)/shard_map/ppermute | solution.py:497
  172.8 2.4 %collective-permute-start.8 = (f32[64,256]{1,0:T(8,128)S(1)}, f32[64,256]{1,0:T(8,128)S(1)}, u32[]{:S(2)}, u32[]{:S(2)}) collective-permute-start(f32[64,256]{1,0:T(8,128)S(1)} %get-tuple-element.57), channel_id=1, source_target_pairs={{0,496},{16,0},{32,16},{48,32},{64,48},{80,64},{96,80},{112,96},{1... | collective-permute-start | bytes 196616 | tf_op jit(solution)/shard_map/ppermute | solution.py:497
  175.2 0.3 collective-permute-done.9.after
  175.5 4.3 %collective-permute-done.8.before = f32[64,256]{1,0:T(8,128)S(1)} collective-permute-done((f32[64,256]{1,0:T(8,128)S(1)}, f32[64,256]{1,0:T(8,128)S(1)}, u32[]{:S(2)}, u32[]{:S(2)}) %collective-permute-start.8) | collective-permute-done | bytes 65568 | tf_op jit(solution)/shard_map/ppermute | solution.py:497
  179.8 0.0 collective-permute-done.5.other
  179.9 1.9 %shard_map.180 = (f32[1,1]{1,0:T(1,128)}, f32[8,8,192]{2,1,0:T(8,128)}, f32[192,256]{1,0:T(8,128)}, f32[1,256]{1,0:T(1,128)}, f32[256,768]{1,0:T(8,128)}, /*inde...) custom-call(s32[1]{0:T(128)} %bitcast.refs_0_.core, ...), custom_call_target="tpu_custom_call" | custom-call | tf_op jit(solution)/shard_map/pallas_call | solution.py:488
  (7 shorter events, 0.1 us)
Async XLA Ops:
  0.6 0.8 copy-start.6
  1.5 0.8 copy-start.7
  2.7 9.7 %collective-permute-start.1 = (f32[64,256]{1,0:T(8,128)S(1)}, f32[64,256]{1,0:T(8,128)S(1)}, u32[]{:S(2)}, u32[]{:S(2)}) collective-permute-start(f32[64,256]{1,0:T(8,128)S(1)} %get-tuple-element.33), channel_id=1, source_target_pairs={{0,496},{16,0},{32,16},{48,32},{64,48},{80,64},{96,80},{112,96},{1... | collective-permute-start | bytes 196616 | tf_op jit(solution)/shard_map/ppermute | solution.py:497
  10.5 9.2 %collective-permute-start = (f32[64,256]{1,0:T(8,128)S(1)}, f32[64,256]{1,0:T(8,128)S(1)}, u32[]{:S(2)}, u32[]{:S(2)}) collective-permute-start(f32[64,256]{1,0:T(8,128)S(1)} %get-tuple-element.33), channel_id=1, source_target_pairs={{0,16},{16,32},{32,48},{48,64},{64,80},{80,96},{96,112},{112,128},... | collective-permute-start | bytes 196616 | tf_op jit(solution)/shard_map/ppermute | solution.py:497
  19.7 15.4 %copy-start.8 = (f32[256]{0:T(256)S(1)}, f32[256]{0:T(256)}, u32[]{:S(2)}) copy-start(f32[256]{0:T(256)} %param.13) | copy-start | bytes 3076
  19.7 15.4 %copy-start.9 = (f32[256]{0:T(256)S(1)}, f32[256]{0:T(256)}, u32[]{:S(2)}) copy-start(f32[256]{0:T(256)} %param.16) | copy-start | bytes 3076
  19.7 13.4 %collective-permute-start.3 = (f32[3,64,256]{2,1,0:T(8,128)S(1)}, f32[3,64,256]{2,1,0:T(8,128)S(1)}, u32[]{:S(2)}, u32[]{:S(2)}) collective-permute-start(f32[3,64,256]{2,1,0:T(8,128)S(1)} %pad_maximum_fusion.refs_2_), channel_id=1, source_target_pairs={{0,15},{1,0},{2,1},{3,2},{4,3},{5,4},{6,5},{7,6},{8,7},{9,8},{10,9... | collective-permute-start | bytes 589832 | tf_op jit(solution)/shard_map/ppermute | solution.py:497
  24.5 10.6 %collective-permute-start.2 = (f32[3,64,256]{2,1,0:T(8,128)S(1)}, f32[3,64,256]{2,1,0:T(8,128)S(1)}, u32[]{:S(2)}, u32[]{:S(2)}) collective-permute-start(f32[3,64,256]{2,1,0:T(8,128)S(1)} %pad_maximum_fusion.refs_2_), channel_id=1, source_target_pairs={{0,1},{1,2},{2,3},{3,4},{4,5},{5,6},{6,7},{7,8},{8,9},{9,10},{10,1... | collective-permute-start | bytes 589832 | tf_op jit(solution)/shard_map/ppermute | solution.py:497
  26.4 1.1 copy-start
  27.6 1.0 copy-start.1
  28.6 1.0 copy-start.2
  29.7 0.9 copy-start.3
  30.6 0.9 copy-start.4
  31.5 0.9 copy-start.5
  62.3 4.9 %collective-permute-start.4 = (f32[1280,256]{1,0:T(8,128)S(1)}, f32[1280,256]{1,0:T(8,128)S(1)}, u32[]{:S(2)}, u32[]{:S(2)}) collective-permute-start(f32[1280,256]{1,0:T(8,128)S(1)} %get-tuple-element.42), channel_id=1, source_target_pairs={{0,1},{1,0},{2,3},{3,2},{4,5},{5,4},{6,7},{7,6},{8,9},{9,8},{10,11... | collective-permute-start | bytes 3932168 | tf_op jit(solution)/shard_map/ppermute | solution.py:516
  152.5 27.3 %collective-permute-start.5 = (f32[1280,256]{1,0:T(8,128)S(1)}, f32[1280,256]{1,0:T(8,128)S(1)}, u32[]{:S(2)}, u32[]{:S(2)}) collective-permute-start(f32[1280,256]{1,0:T(8,128)S(1)} %bitcast.17), channel_id=1, source_target_pairs={{0,1},{1,0},{2,3},{3,2},{4,5},{5,4},{6,7},{7,6},{8,9},{9,8},{10,11... | collective-permute-start | bytes 3932168 | tf_op jit(solution)/shard_map/ppermute | solution.py:524
  154.4 7.4 %collective-permute-start.6 = (f32[3,64,256]{2,1,0:T(8,128)S(1)}, f32[3,64,256]{2,1,0:T(8,128)S(1)}, u32[]{:S(2)}, u32[]{:S(2)}) collective-permute-start(f32[3,64,256]{2,1,0:T(8,128)S(1)} %get-tuple-element.44), channel_id=1, source_target_pairs={{0,15},{1,0},{2,1},{3,2},{4,3},{5,4},{6,5},{7,6},{8,7},{9,8},{10,9... | collective-permute-start | bytes 589832 | tf_op jit(solution)/shard_map/ppermute | solution.py:497
  158.7 10.6 %collective-permute-start.7 = (f32[3,64,256]{2,1,0:T(8,128)S(1)}, f32[3,64,256]{2,1,0:T(8,128)S(1)}, u32[]{:S(2)}, u32[]{:S(2)}) collective-permute-start(f32[3,64,256]{2,1,0:T(8,128)S(1)} %get-tuple-element.45), channel_id=1, source_target_pairs={{0,1},{1,2},{2,3},{3,4},{4,5},{5,6},{6,7},{7,8},{8,9},{9,10},{10,1... | collective-permute-start | bytes 589832 | tf_op jit(solution)/shard_map/ppermute | solution.py:497
  169.3 6.2 %collective-permute-start.9 = (f32[64,256]{1,0:T(8,128)S(1)}, f32[64,256]{1,0:T(8,128)S(1)}, u32[]{:S(2)}, u32[]{:S(2)}) collective-permute-start(f32[64,256]{1,0:T(8,128)S(1)} %get-tuple-element.56), channel_id=1, source_target_pairs={{0,16},{16,32},{32,48},{48,64},{64,80},{80,96},{96,112},{112,128},... | collective-permute-start | bytes 196616 | tf_op jit(solution)/shard_map/ppermute | solution.py:497
  172.8 7.1 %collective-permute-start.8 = (f32[64,256]{1,0:T(8,128)S(1)}, f32[64,256]{1,0:T(8,128)S(1)}, u32[]{:S(2)}, u32[]{:S(2)}) collective-permute-start(f32[64,256]{1,0:T(8,128)S(1)} %get-tuple-element.57), channel_id=1, source_target_pairs={{0,496},{16,0},{32,16},{48,32},{64,48},{80,64},{96,80},{112,96},{1... | collective-permute-start | bytes 196616 | tf_op jit(solution)/shard_map/ppermute | solution.py:497

commit v4 on v3

--- a/solution.py
+++ b/solution.py
@@ -38,7 +38,7 @@
     return x + pltpu.roll(x, 64, 1)
 
 
-def to_tokens(block_ref, rows_ref, turned_ref, out_ref):
+def to_tokens(block_ref, out_ref, rows_ref, turned_ref):
     for px in range(2):
         for py in range(2):
             for dx in range(4):
@@ -61,11 +61,6 @@
     for column in range(4):
         for half in range(2):
             out_ref[column * 16 : column * 16 + 16, half * 128 : half * 128 + 128] = halves[column][half]
-
-
-def prepare_kernel(field_ref, target_ref, tokens_ref, goal_ref, rows_ref, turned_ref):
-    to_tokens(field_ref, rows_ref, turned_ref, tokens_ref)
-    to_tokens(target_ref, rows_ref, turned_ref, goal_ref)
 
 
 def from_tokens(total, out_ref, turned_ref, rows_ref):
@@ -351,7 +346,11 @@
     add_inner(back_ref, m, n, dmid)
     dtokens = split(back_ref[...])
     add_rows(grads, EMBED, dot(split(ext_ref[...]), dtokens, 0, 0)[:192], first)
-    back_ref[...] = dot(dtokens, both(w["embed"]), 1, 1)
+    return dtokens
+
+
+def backward_field(embed, ext_ref, back_ref, dtokens, g, m, n):
+    back_ref[...] = dot(dtokens, both(embed), 1, 1)
     stencil_back(ext_ref, back_ref, g, m, n)
 
 
@@ -369,32 +368,40 @@
             put(w[name], 0, inputs[name][...])
 
 
+SPOTS = [
+    (by, bx, (px * 2 + py) * 16, ((2 * bx + px) * 6 + 2 * by + py) * 16)
+    for by in range(3) for bx in range(3) for px in range(2) for py in range(2)
+]
+
+
+def field_kernel(embed, ext0, g0, dtokens, out_low, out_own, out_high, back_ref):
+    backward_field(embed, ext0, back_ref, both(dtokens), g0[...], 6, 4)
+    for by, bx, source, place in SPOTS:
+        (out_low, out_own, out_high)[by][bx, source : source + 16, :] = back_ref[place : place + 16, :]
+
+
 def main_kernel(*refs):
     (core, low, own, high, goal, gain1, gain2) = refs[:7]
     w = dict(zip(NAMES, refs[7:13]))
-    (kept, sent, out_low, out_own, out_high) = refs[13:18]
+    (kept, sent, ext0, g0, dtokens0) = refs[13:18]
     scratch = list(refs[18:])
     grads = scratch.pop(0)
-    ext0, back0, ext1, back1, dkv0, dkv1, dq0, dq1 = scratch[:8]
-    r0, r1 = scratch[8:17], scratch[17:26]
+    back0, ext1, back1, dkv0, dkv1, dq0, dq1 = scratch[:7]
+    r0, r1 = scratch[7:16], scratch[16:25]
     g1, g2 = gain1[...], gain2[...]
-    spots = [
-        (by, bx, (px * 2 + py) * 16, ((2 * bx + px) * 6 + 2 * by + py) * 16)
-        for by in range(3) for bx in range(3) for px in range(2) for py in range(2)
-    ]
-    for by, bx, source, place in spots:
+    for by, bx, source, place in SPOTS:
         ext0[place : place + 16, :] = (low, own, high)[by][bx, source : source + 16, :]
-    ext1[...] = stencil(ext0, 6, 4) + 0.1 * forward(w, g1, g2, ext0, r0, 6, 4, 192)
-    final = stencil(ext1, 4, 2) + 0.1 * forward(w, g1, g2, ext1, r1, 4, 2, 128)
+    ext1[...] = stencil(ext0, 6, 4) + 0.1 * forward(w, g1, g2, ext0, r0, 6, 4, 576)
+    final = stencil(ext1, 4, 2) + 0.1 * forward(w, g1, g2, ext1, r1, 4, 2, 256)
     residue = final - goal[...]
     grads[SMALL:ROWS, :] = jnp.zeros((ROWS - SMALL, 256), F32)
     sums = [jnp.sum(jnp.sum(v * v, axis=0, keepdims=True), axis=1, keepdims=True) for v in (residue, goal[...])]
     lane = lanes((1, 256))
     grads[SMALL + 2 : SMALL + 3, :] = jnp.where(lane == 0, sums[0], jnp.where(lane == 1, sums[1], 0.0))
-    backward(w, g1, g2, ext1, back1, grads, r1, dkv1, dq1, 2.0 * residue, 4, 2, True)
-    backward(w, g1, g2, ext0, back0, grads, r0, dkv0, dq0, back1[...], 6, 4, False)
-    for by, bx, source, place in spots:
-        (out_low, out_own, out_high)[by][bx, source : source + 16, :] = back0[place : place + 16, :]
+    g = 2.0 * residue
+    dtokens = backward(w, g1, g2, ext1, back1, grads, r1, dkv1, dq1, g, 4, 2, True)
+    backward_field(w["embed"], ext1, g0, dtokens, g, 4, 2)
+    dtokens0[0], dtokens0[1] = backward(w, g1, g2, ext0, back0, grads, r0, dkv0, dq0, g0[...], 6, 4, False)
     half = ROWS // 2
     kept[...] = grads[pl.ds(pl.multiple_of(core[0] * half, half), half), :]
     sent[...] = grads[pl.ds(pl.multiple_of((1 - core[0]) * half, half), half), :]
@@ -443,9 +450,9 @@
     )
 
 
-def prepare(field, target):
+def prepare(block):
     scratch = [pltpu.VMEM((64, 192), F32), pltpu.VMEM((192, 128), F32)]
-    return call(prepare_kernel, (arr(64, 256), arr(64, 256)), scratch, 4)(field, target)
+    return call(to_tokens, arr(64, 256), scratch, 4)(block)
 
 
 def split_weights(weights):
@@ -467,13 +474,18 @@
 
     scratch = [
         V(ROWS, 256),
-        V(576, 256), V(576, 256), V(256, 256), V(256, 256), V(576, 512), V(256, 512), V(256, 256), V(64, 256),
+        V(576, 256), V(256, 256), V(256, 256), V(576, 512), V(256, 512), V(256, 256), V(64, 256),
         *kept(576, 256, 4), *kept(256, 64, 2),
     ]
     half = arr(ROWS // 2, 256)
-    outs = (half, half, arr(3, 64, 256), arr(3, 64, 256), arr(3, 64, 256))
+    outs = (half, half, arr(576, 256), arr(256, 256), arr(2, 576, 256, dtype=BF16))
     args = (gains[0].reshape(1, 256), gains[1].reshape(1, 256), *halves)
     return call(main_kernel, outs, scratch, 24, in_specs=places(1, 12))(core, low, own, high, goal, *args)
+
+
+def adjoint(embed, ext0, g0, dtokens):
+    outs = [arr(3, 64, 256)] * 3
+    return call(field_kernel, outs, [pltpu.VMEM((576, 256), F32)], 10)(embed, ext0, g0, dtokens)
 
 
 def finish(core, mine, other, wide, before, after):
@@ -509,11 +521,13 @@
     half = ROWS // 2
     swapped = [(0, 1), (1, 0)]
     halves = split_weights(weights)
-    tokens, goal = prepare(field, target)
+    tokens = prepare(field)
+    goal = prepare(target)
     own = jnp.stack([shift(tokens, GX, 1), tokens, shift(tokens, GX, -1)])
     low, high = shift(own, GY, 1), shift(own, GY, -1)
-    kept, sent, back_low, back_own, back_high = work(core, low, own, high, goal, (weights[1], weights[4]), halves)
+    kept, sent, ext0, g0, dtokens = work(core, low, own, high, goal, (weights[1], weights[4]), halves)
     total = kept + lax.ppermute(sent, "co", swapped)
+    back_low, back_own, back_high = adjoint(halves[0], ext0, g0, dtokens)
     back_low, back_high = shift(back_low, GY, -1), shift(back_high, GY, 1)
     wide = back_own + (back_low + back_high)
     total = jnp.sum(swap(total.reshape(16, half // 16, 256), PLANE), axis=0)

time: 183 us -> 180 us (0.984)
  Pallas kernels: 30.1 us -> 27.7 us
    pallas_call x1, Pallas kernels: 27.2 us -> 22.2 us  [work(): call(main_kernel, outs, scratch, 24, in_specs=places(1, 12))]
    pallas_call x1 -> x3, Pallas kernels: 0.34 us -> 2.85 us  [the longest x1 2.35 us: adjoint(): call(field_kernel, outs, [pltpu.VMEM((576, 256), F32)], 10)]
  transfers between devices with their start and end apart: 10 -> 10, of which waited for: 7 -> 7; matrix products, arithmetic and copies ran while one was open for 0% -> 0% of each run, Pallas kernels for 0% -> 2%
where the time goes in v4:
time: 180 us; the launch traced here: 179 us
  blocking collectives  85.9 us (48%)
  starting transfers between devices  32.2 us (18%)
  Pallas kernels  27.7 us (15%)
  waiting for transfers between devices  24.5 us (14%)
  local copies, waits for them, and re-layouts  7.86 us (4%)
    all_to_all x4, blocking collectives, swap(): return lax.all_to_all(x, axes, 0, 0, tiled=True)  85.9 us
    ppermute x8, starting transfers between devices, shift(): lax.ppermute(x, axes, [(i, (i + step) % count) for i in range(count)])  28.4 us
    pallas_call x1, Pallas kernels, work(): call(main_kernel, outs, scratch, 24, in_specs=places(1, 12))  22.2 us
    ppermute x8, waiting for transfers between devices, shift(): lax.ppermute(x, axes, [(i, (i + step) % count) for i in range(count)])  21.5 us
    unnamed x20, local copies, waits for them, and re-layouts  7.69 us
  transfers between devices with their start and end apart: 10, of which 7 were waited for; matrix products, arithmetic and copies ran while one was open for 0% of the time, Pallas kernels for 2%

profile of v4, /device:TPU:2, one launch (start us, length us, event | category | flops | bytes accessed | tf_op | source)
XLA Modules:
  0.0 179.4 jit_solution(3472029765099355138)
XLA Ops:
  0.6 0.0 copy-start.6
  0.7 0.8 copy-done.6
  1.5 0.3 shard_map.177
  1.7 7.8 %collective-permute-start.1 = (f32[64,256]{1,0:T(8,128)S(1)}, f32[64,256]{1,0:T(8,128)S(1)}, u32[]{:S(2)}, u32[]{:S(2)}) collective-permute-start(f32[64,256]{1,0:T(8,128)S(1)} %shard_map.177), channel_id=1, source_target_pairs={{0,496},{16,0},{32,16},{48,32},{64,48},{80,64},{96,80},{112,96},{1... | collective-permute-start | bytes 196616 | tf_op jit(solution)/shard_map/ppermute | solution.py:509
  9.5 1.9 %collective-permute-start = (f32[64,256]{1,0:T(8,128)S(1)}, f32[64,256]{1,0:T(8,128)S(1)}, u32[]{:S(2)}, u32[]{:S(2)}) collective-permute-start(f32[64,256]{1,0:T(8,128)S(1)} %shard_map.177), channel_id=1, source_target_pairs={{0,16},{16,32},{32,48},{48,64},{64,80},{80,96},{96,112},{112,128},... | collective-permute-start | bytes 196616 | tf_op jit(solution)/shard_map/ppermute | solution.py:509
  11.5 0.0 collective-permute-done.1
  11.5 7.3 %collective-permute-done = f32[64,256]{1,0:T(8,128)S(1)} collective-permute-done((f32[64,256]{1,0:T(8,128)S(1)}, f32[64,256]{1,0:T(8,128)S(1)}, u32[]{:S(2)}, u32[]{:S(2)}) %collective-permute-start) | collective-permute-done | bytes 65568 | tf_op jit(solution)/shard_map/ppermute | solution.py:509
  18.8 4.8 %collective-permute-start.3 = (f32[3,64,256]{2,1,0:T(8,128)S(1)}, f32[3,64,256]{2,1,0:T(8,128)S(1)}, u32[]{:S(2)}, u32[]{:S(2)}) collective-permute-start(f32[3,64,256]{2,1,0:T(8,128)S(1)} %pad_maximum_fusion.refs_2_), channel_id=1, source_target_pairs={{0,15},{1,0},{2,1},{3,2},{4,3},{5,4},{6,5},{7,6},{8,7},{9,8},{10,9... | collective-permute-start | bytes 589832 | tf_op jit(solution)/shard_map/ppermute | solution.py:509
  23.6 1.9 %collective-permute-start.2 = (f32[3,64,256]{2,1,0:T(8,128)S(1)}, f32[3,64,256]{2,1,0:T(8,128)S(1)}, u32[]{:S(2)}, u32[]{:S(2)}) collective-permute-start(f32[3,64,256]{2,1,0:T(8,128)S(1)} %pad_maximum_fusion.refs_2_), channel_id=1, source_target_pairs={{0,1},{1,2},{2,3},{3,4},{4,5},{5,6},{6,7},{7,8},{8,9},{9,10},{10,1... | collective-permute-start | bytes 589832 | tf_op jit(solution)/shard_map/ppermute | solution.py:509
  25.5 0.0 copy-start.7
  25.5 0.8 copy-done.7
  26.3 0.0 copy-start.8
  26.3 0.0 copy-start.9
  26.3 0.3 shard_map.178.refs_4_
  26.6 0.0 copy-start
  26.6 1.1 copy-done
  27.7 0.0 copy-start.1
  27.7 1.0 copy-done.1
  28.8 0.0 copy-start.2
  28.8 1.0 copy-done.2
  29.8 0.0 copy-start.3
  29.8 0.9 copy-done.3
  30.8 0.0 copy-start.4
  30.8 0.9 copy-done.4
  31.7 0.0 copy-start.5
  31.7 0.9 copy-done.5
  32.6 0.6 shard_map.179
  33.3 0.0 collective-permute-done.3.refs_3_
  33.3 0.9 collective-permute-done.2.refs_1_
  34.2 0.0 copy-done.8
  34.2 0.0 copy-done.9
  34.2 22.2 %shard_map.180 = (f32[1280,256]{1,0:T(8,128)S(1)}, f32[1280,256]{1,0:T(8,128)S(1)}, f32[576,256]{1,0:T(8,128)S(1)}, f32[256,256]{1,0:T(8,128)S(1)}, bf16[2,576,256]{2,1,0:T(8,128)(2,1)S(1)}) custom-call(s32[1]{0:T(128)} %bitcast.refs_0_.core, f32[3,64,256]{2,1,0:T(8,128)S(1)} %collective-permute-done.2.refs_1_, f32[3,64,256]{2,1,0:T(8,128)S(1)} %pad_maximum_fusion.refs_2_, ...), custom_call_target="tpu_custom_call" | custom-call | tf_op jit(solution)/shard_map/pallas_call | solution.py:483
  56.4 1.9 %collective-permute-start.4 = (f32[1280,256]{1,0:T(8,128)S(1)}, f32[1280,256]{1,0:T(8,128)S(1)}, u32[]{:S(2)}, u32[]{:S(2)}) collective-permute-start(f32[1280,256]{1,0:T(8,128)S(1)} %get-tuple-element.41), channel_id=1, source_target_pairs={{0,1},{1,0},{2,3},{3,2},{4,5},{5,4},{6,7},{7,6},{8,9},{9,8},{10,11... | collective-permute-start | bytes 3932168 | tf_op jit(solution)/shard_map/ppermute | solution.py:529
  58.3 3.0 %collective-permute-done.4 = f32[1280,256]{1,0:T(8,128)S(1)} collective-permute-done((f32[1280,256]{1,0:T(8,128)S(1)}, f32[1280,256]{1,0:T(8,128)S(1)}, u32[]{:S(2)}, u32[]{:S(2)}) %collective-permute-start.4) | collective-permute-done | bytes 1310752 | tf_op jit(solution)/shard_map/ppermute | solution.py:529
  61.3 0.2 add.9
  61.5 29.2 %all_to_all.20 = f32[16,80,256]{2,1,0:T(8,128)S(1)} all-to-all(f32[16,80,256]{2,1,0:T(8,128)S(1)} %bitcast.23), channel_id=1, replica_groups=mesh['z'=16,'xl'=2,'y'=4,'xh'=2,'co'=2] {'xl','y','xh'}, dimensions={0} | all-to-all | bytes 2621440 | tf_op jit(solution)/shard_map/all_to_all | solution.py:516
  90.7 0.1 reduce_sum.18
  90.8 19.5 %all_to_all.21 = f32[16,5,256]{2,1,0:T(8,128)S(1)} all-to-all(f32[16,5,256]{2,1,0:T(8,128)S(1)} %reshape.45), channel_id=1, replica_groups=mesh['z'=16,'xl'=2,'y'=4,'xh'=2,'co'=2] {'z'}, dimensions={0} | all-to-all | bytes 163840 | tf_op jit(solution)/shard_map/all_to_all | solution.py:516
  110.4 16.5 %all_to_all.22 = f32[16,5,256]{2,1,0:T(8,128)S(1)} all-to-all(f32[16,5,256]{2,1,0:T(8,128)S(1)} %broadcast_in_dim.6), channel_id=1, replica_groups=mesh['z'=16,'xl'=2,'y'=4,'xh'=2,'co'=2] {'z'}, dimensions={0} | all-to-all | bytes 163840 | tf_op jit(solution)/shard_map/all_to_all | solution.py:516
  126.9 0.1 broadcast_in_dim.7
  127.0 20.7 %all_to_all.23 = f32[16,80,256]{2,1,0:T(8,128)S(1)} all-to-all(f32[16,80,256]{2,1,0:T(8,128)S(1)} %broadcast_in_dim.7), channel_id=1, replica_groups=mesh['z'=16,'xl'=2,'y'=4,'xh'=2,'co'=2] {'xl','y','xh'}, dimensions={0} | all-to-all | bytes 2621440 | tf_op jit(solution)/shard_map/all_to_all | solution.py:516
  147.7 1.9 %collective-permute-start.5 = (f32[1280,256]{1,0:T(8,128)S(1)}, f32[1280,256]{1,0:T(8,128)S(1)}, u32[]{:S(2)}, u32[]{:S(2)}) collective-permute-start(f32[1280,256]{1,0:T(8,128)S(1)} %bitcast.17), channel_id=1, source_target_pairs={{0,1},{1,0},{2,3},{3,2},{4,5},{5,4},{6,7},{7,6},{8,9},{9,8},{10,11... | collective-permute-start | bytes 3932168 | tf_op jit(solution)/shard_map/ppermute | solution.py:538
  149.6 2.3 %shard_map.181 = (f32[3,64,256]{2,1,0:T(8,128)S(1)}, f32[3,64,256]{2,1,0:T(8,128)S(1)}, f32[3,64,256]{2,1,0:T(8,128)S(1)}) custom-call(bf16[2,256,256]{2,1,0:T(8,128)(2,1)S(1)} %get-tuple-element.34.refs_7_.embed, f32[576,256]{1,0:T(8,128)S(1)} %get-tuple-element.42.ext0, f32[256,256]{1,0:T(8,128)S(1)} %get-tuple-element.43.g0, ...), custom_call_target="tpu_custom_call" | custom-call | tf_op jit(solution)/shard_map/pallas_call | solution.py:488
  152.0 4.2 %collective-permute-start.6 = (f32[3,64,256]{2,1,0:T(8,128)S(1)}, f32[3,64,256]{2,1,0:T(8,128)S(1)}, u32[]{:S(2)}, u32[]{:S(2)}) collective-permute-start(f32[3,64,256]{2,1,0:T(8,128)S(1)} %get-tuple-element.46), channel_id=1, source_target_pairs={{0,15},{1,0},{2,1},{3,2},{4,3},{5,4},{6,5},{7,6},{8,7},{9,8},{10,9... | collective-permute-start | bytes 589832 | tf_op jit(solution)/shard_map/ppermute | solution.py:509
  156.3 1.9 %collective-permute-start.7 = (f32[3,64,256]{2,1,0:T(8,128)S(1)}, f32[3,64,256]{2,1,0:T(8,128)S(1)}, u32[]{:S(2)}, u32[]{:S(2)}) collective-permute-start(f32[3,64,256]{2,1,0:T(8,128)S(1)} %get-tuple-element.47), channel_id=1, source_target_pairs={{0,1},{1,2},{2,3},{3,4},{4,5},{5,6},{6,7},{7,8},{8,9},{9,10},{10,1... | collective-permute-start | bytes 589832 | tf_op jit(solution)/shard_map/ppermute | solution.py:509
  158.2 1.2 collective-permute-done.6
  159.4 7.4 %collective-permute-done.7 = f32[3,64,256]{2,1,0:T(8,128)S(1)} collective-permute-done((f32[3,64,256]{2,1,0:T(8,128)S(1)}, f32[3,64,256]{2,1,0:T(8,128)S(1)}, u32[]{:S(2)}, u32[]{:S(2)}) %collective-permute-start.7) | collective-permute-done | bytes 196640 | tf_op jit(solution)/shard_map/ppermute | solution.py:509
  166.9 3.4 %collective-permute-start.9 = (f32[64,256]{1,0:T(8,128)S(1)}, f32[64,256]{1,0:T(8,128)S(1)}, u32[]{:S(2)}, u32[]{:S(2)}) collective-permute-start(f32[64,256]{1,0:T(8,128)S(1)} %get-tuple-element.58), channel_id=1, source_target_pairs={{0,16},{16,32},{32,48},{48,64},{64,80},{80,96},{96,112},{112,128},... | collective-permute-start | bytes 196616 | tf_op jit(solution)/shard_map/ppermute | solution.py:509
  170.4 2.4 %collective-permute-start.8 = (f32[64,256]{1,0:T(8,128)S(1)}, f32[64,256]{1,0:T(8,128)S(1)}, u32[]{:S(2)}, u32[]{:S(2)}) collective-permute-start(f32[64,256]{1,0:T(8,128)S(1)} %get-tuple-element.59), channel_id=1, source_target_pairs={{0,496},{16,0},{32,16},{48,32},{64,48},{80,64},{96,80},{112,96},{1... | collective-permute-start | bytes 196616 | tf_op jit(solution)/shard_map/ppermute | solution.py:509
  172.8 0.3 collective-permute-done.9.after
  173.1 4.3 %collective-permute-done.8.before = f32[64,256]{1,0:T(8,128)S(1)} collective-permute-done((f32[64,256]{1,0:T(8,128)S(1)}, f32[64,256]{1,0:T(8,128)S(1)}, u32[]{:S(2)}, u32[]{:S(2)}) %collective-permute-start.8) | collective-permute-done | bytes 65568 | tf_op jit(solution)/shard_map/ppermute | solution.py:509
  177.4 0.0 collective-permute-done.5.other
  177.4 1.9 %shard_map.182 = (f32[1,1]{1,0:T(1,128)}, f32[8,8,192]{2,1,0:T(8,128)}, f32[192,256]{1,0:T(8,128)}, f32[1,256]{1,0:T(1,128)}, f32[256,768]{1,0:T(8,128)}, /*inde...) custom-call(s32[1]{0:T(128)} %bitcast.refs_0_.core, ...), custom_call_target="tpu_custom_call" | custom-call | tf_op jit(solution)/shard_map/pallas_call | solution.py:500
  (7 shorter events, 0.1 us)
Async XLA Ops:
  0.6 0.8 copy-start.6
  1.7 9.7 %collective-permute-start.1 = (f32[64,256]{1,0:T(8,128)S(1)}, f32[64,256]{1,0:T(8,128)S(1)}, u32[]{:S(2)}, u32[]{:S(2)}) collective-permute-start(f32[64,256]{1,0:T(8,128)S(1)} %shard_map.177), channel_id=1, source_target_pairs={{0,496},{16,0},{32,16},{48,32},{64,48},{80,64},{96,80},{112,96},{1... | collective-permute-start | bytes 196616 | tf_op jit(solution)/shard_map/ppermute | solution.py:509
  9.5 9.2 %collective-permute-start = (f32[64,256]{1,0:T(8,128)S(1)}, f32[64,256]{1,0:T(8,128)S(1)}, u32[]{:S(2)}, u32[]{:S(2)}) collective-permute-start(f32[64,256]{1,0:T(8,128)S(1)} %shard_map.177), channel_id=1, source_target_pairs={{0,16},{16,32},{32,48},{48,64},{64,80},{80,96},{96,112},{112,128},... | collective-permute-start | bytes 196616 | tf_op jit(solution)/shard_map/ppermute | solution.py:509
  18.8 14.5 %collective-permute-start.3 = (f32[3,64,256]{2,1,0:T(8,128)S(1)}, f32[3,64,256]{2,1,0:T(8,128)S(1)}, u32[]{:S(2)}, u32[]{:S(2)}) collective-permute-start(f32[3,64,256]{2,1,0:T(8,128)S(1)} %pad_maximum_fusion.refs_2_), channel_id=1, source_target_pairs={{0,15},{1,0},{2,1},{3,2},{4,3},{5,4},{6,5},{7,6},{8,7},{9,8},{10,9... | collective-permute-start | bytes 589832 | tf_op jit(solution)/shard_map/ppermute | solution.py:509
  23.6 10.6 %collective-permute-start.2 = (f32[3,64,256]{2,1,0:T(8,128)S(1)}, f32[3,64,256]{2,1,0:T(8,128)S(1)}, u32[]{:S(2)}, u32[]{:S(2)}) collective-permute-start(f32[3,64,256]{2,1,0:T(8,128)S(1)} %pad_maximum_fusion.refs_2_), channel_id=1, source_target_pairs={{0,1},{1,2},{2,3},{3,4},{4,5},{5,6},{6,7},{7,8},{8,9},{9,10},{10,1... | collective-permute-start | bytes 589832 | tf_op jit(solution)/shard_map/ppermute | solution.py:509
  25.5 0.8 copy-start.7
  26.3 7.8 %copy-start.8 = (f32[256]{0:T(256)S(1)}, f32[256]{0:T(256)}, u32[]{:S(2)}) copy-start(f32[256]{0:T(256)} %param.13) | copy-start | bytes 3076
  26.3 7.8 %copy-start.9 = (f32[256]{0:T(256)S(1)}, f32[256]{0:T(256)}, u32[]{:S(2)}) copy-start(f32[256]{0:T(256)} %param.16) | copy-start | bytes 3076
  26.6 1.1 copy-start
  27.7 1.0 copy-start.1
  28.8 1.0 copy-start.2
  29.8 0.9 copy-start.3
  30.8 0.9 copy-start.4
  31.7 0.9 copy-start.5
  56.4 4.9 %collective-permute-start.4 = (f32[1280,256]{1,0:T(8,128)S(1)}, f32[1280,256]{1,0:T(8,128)S(1)}, u32[]{:S(2)}, u32[]{:S(2)}) collective-permute-start(f32[1280,256]{1,0:T(8,128)S(1)} %get-tuple-element.41), channel_id=1, source_target_pairs={{0,1},{1,0},{2,3},{3,2},{4,5},{5,4},{6,7},{7,6},{8,9},{9,8},{10,11... | collective-permute-start | bytes 3932168 | tf_op jit(solution)/shard_map/ppermute | solution.py:529
  147.7 29.7 %collective-permute-start.5 = (f32[1280,256]{1,0:T(8,128)S(1)}, f32[1280,256]{1,0:T(8,128)S(1)}, u32[]{:S(2)}, u32[]{:S(2)}) collective-permute-start(f32[1280,256]{1,0:T(8,128)S(1)} %bitcast.17), channel_id=1, source_target_pairs={{0,1},{1,0},{2,3},{3,2},{4,5},{5,4},{6,7},{7,6},{8,9},{9,8},{10,11... | collective-permute-start | bytes 3932168 | tf_op jit(solution)/shard_map/ppermute | solution.py:538
  152.0 7.4 %collective-permute-start.6 = (f32[3,64,256]{2,1,0:T(8,128)S(1)}, f32[3,64,256]{2,1,0:T(8,128)S(1)}, u32[]{:S(2)}, u32[]{:S(2)}) collective-permute-start(f32[3,64,256]{2,1,0:T(8,128)S(1)} %get-tuple-element.46), channel_id=1, source_target_pairs={{0,15},{1,0},{2,1},{3,2},{4,3},{5,4},{6,5},{7,6},{8,7},{9,8},{10,9... | collective-permute-start | bytes 589832 | tf_op jit(solution)/shard_map/ppermute | solution.py:509
  156.3 10.6 %collective-permute-start.7 = (f32[3,64,256]{2,1,0:T(8,128)S(1)}, f32[3,64,256]{2,1,0:T(8,128)S(1)}, u32[]{:S(2)}, u32[]{:S(2)}) collective-permute-start(f32[3,64,256]{2,1,0:T(8,128)S(1)} %get-tuple-element.47), channel_id=1, source_target_pairs={{0,1},{1,2},{2,3},{3,4},{4,5},{5,6},{6,7},{7,8},{8,9},{9,10},{10,1... | collective-permute-start | bytes 589832 | tf_op jit(solution)/shard_map/ppermute | solution.py:509
  166.9 6.2 %collective-permute-start.9 = (f32[64,256]{1,0:T(8,128)S(1)}, f32[64,256]{1,0:T(8,128)S(1)}, u32[]{:S(2)}, u32[]{:S(2)}) collective-permute-start(f32[64,256]{1,0:T(8,128)S(1)} %get-tuple-element.58), channel_id=1, source_target_pairs={{0,16},{16,32},{32,48},{48,64},{64,80},{80,96},{96,112},{112,128},... | collective-permute-start | bytes 196616 | tf_op jit(solution)/shard_map/ppermute | solution.py:509
  170.4 7.1 %collective-permute-start.8 = (f32[64,256]{1,0:T(8,128)S(1)}, f32[64,256]{1,0:T(8,128)S(1)}, u32[]{:S(2)}, u32[]{:S(2)}) collective-permute-start(f32[64,256]{1,0:T(8,128)S(1)} %get-tuple-element.59), channel_id=1, source_target_pairs={{0,496},{16,0},{32,16},{48,32},{64,48},{80,64},{96,80},{112,96},{1... | collective-permute-start | bytes 196616 | tf_op jit(solution)/shard_map/ppermute | solution.py:509
